TPU v7x, 512 devices: a whole 4x8x8 slice. The times are simulated.
512 devices in a mesh: seq: 8 (over z), mp: 16 (over y, core), dp: 4 (over x).
Axes of the slice: x: 4, y: 8, z: 8, core: 2. Of those that a mesh axis runs over, the one named last changes fastest.
Arguments:
- tokens: bfloat16 [65536, 2048], P(('dp', 'seq'), 'mp'), parts along dimension 0, may hold values from -6 to 6
- w_query: bfloat16 [2048, 2048], P(None, 'mp'), may hold values from -0.125 to 0.125
- w_key: bfloat16 [2048, 2048], P(None, 'mp'), may hold values from -0.125 to 0.125
- w_value: bfloat16 [2048, 2048], P(None, 'mp'), may hold values from -0.125 to 0.125
- w_gate: bfloat16 [2048, 2048], P(None, 'mp'), may hold values from -0.125 to 0.125
- decay_exponent: int32 [16], P('mp'), may hold values from 5 to 16
- forget: float32 [65536, 16], P(('dp', 'seq'), 'mp'), parts along dimension 0, may hold values from 0 to 0.69
- norm_gain: float32 [2048], replicated, may hold values from 0.1 to 1.9
Outputs:
- retained: bfloat16 [65536, 2048], P(('dp', 'seq', 'mp')), parts along dimension 0
There are 4 independent parts, one for each index of `dp`. A program takes and returns all parts, laid end to end along the dimension named above; an argument that names none is the same for every part. Nothing has to cross between parts.
All inputs are finite; a program needn't handle non-finite values.
Results may differ from a plain program's by a relative error of at most 0.015.
Values may be sent and summed in bfloat16 or wider, within the bound.
A program may use at most 64 MiB of HBM per device.

v0:
```python
import jax
import jax.numpy as jnp
from jax import lax
from jax.sharding import PartitionSpec as P

HEADS = 16
DH = 128


def from_everyone(shard, axis):
    copies = jnp.broadcast_to(shard, (lax.axis_size(axis), *shard.shape))
    return lax.all_to_all(copies, axis, split_axis=0, concat_axis=0, tiled=True)


def collected_together(shard, axis):
    leaves = jax.tree.leaves(shard)
    sequence = sorted(range(len(leaves)), key=lambda k: -leaves[k].size)
    width = (1, *leaves[sequence[0]].shape)[-1]
    lines = [
        jnp.pad(leaves[k].reshape(-1), (0, -leaves[k].size % width)).reshape(-1, width)
        for k in sequence
    ]
    both, at, found = (from_everyone(jnp.concatenate(lines), axis), 0, {})
    for k, line in zip(sequence, lines):
        section = both[:, at : at + len(line)].reshape(len(both), -1)
        found[k] = section[:, : leaves[k].size].reshape(-1, *leaves[k].shape)
        at += len(line)
    numbers = iter(range(len(leaves)))
    return jax.tree.map(lambda _: found[next(numbers)], shard)


def folded_in_pairs(pieces, combine):
    while len(jax.tree.leaves(pieces)[0]) > 1:
        pieces = jax.vmap(combine)(
            *(jax.tree.map(lambda part: part[side::2], pieces) for side in (0, 1))
        )
    return jax.tree.map(lambda part: part[0], pieces)


def prefix_2(shard, axis, combine, identity):
    size, index = (lax.axis_size(axis), lax.axis_index(axis))
    passed = jnp.arange(size) < index

    def kept(part, zero, own):
        part = jnp.where(
            passed.reshape(-1, *(1 for _ in own.shape)),
            part.astype(own.dtype),
            jnp.asarray(zero, own.dtype),
        )
        return part

    pieces = collected_together(
        jax.tree.map(lambda part, kind: part.astype(kind), shard, (jnp.bfloat16, jnp.bfloat16)),
        axis,
    )
    return folded_in_pairs(jax.tree.map(kept, pieces, identity, shard), combine)


def over_copies(shard, axis):
    return from_everyone(shard, axis).sum(axis=0)


def run_blocks(queries, key_rows, values, logdecay, head_count, head_width):
    seq_rows = queries.shape[0]
    block_rows = 512
    block_count = seq_rows // block_rows

    def shaped(source):
        return source.reshape(block_count, block_rows, head_count, head_width)

    decays = logdecay.reshape(block_count, block_rows, head_count)
    position = lax.broadcasted_iota(jnp.int32, (block_rows, block_rows), 0)
    earlier = lax.broadcasted_iota(jnp.int32, (block_rows, block_rows), 1)
    causal = position >= earlier

    def advance(carried, pieces):
        kv_state, offset = carried
        query_blk, key_blk, value_blk, decay_blk = pieces
        running = jnp.cumsum(decay_blk, axis=0)
        heads_first = running.T
        log_gap = heads_first[:, :, None] - heads_first[:, None, :]
        decay_mask = jnp.where(causal[None], jnp.exp(jnp.where(causal[None], log_gap, 0.0)), 0.0)
        scores = jnp.einsum("tha,sha->hts", query_blk, key_blk, preferred_element_type=jnp.float32)
        scores = (scores * decay_mask).astype(jnp.bfloat16)
        inner = jnp.einsum("hts,shb->thb", scores, value_blk, preferred_element_type=jnp.float32)
        query_float = query_blk.astype(jnp.float32)
        earlier_part = jnp.einsum(
            "tha,hab->thb", query_float * jnp.exp(running)[:, :, None], kv_state
        )
        query_device = query_float * jnp.exp(running + offset[None, :])[:, :, None]
        key_scaled = key_blk.astype(jnp.float32) * jnp.exp(running[-1:] - running)[:, :, None]
        kv_state = jnp.exp(running[-1])[:, None, None] * kv_state + jnp.einsum(
            "sha,shb->hab", key_scaled, value_blk.astype(jnp.float32)
        )
        return ((kv_state, offset + running[-1]), (inner + earlier_part, query_device))

    initial = (
        jnp.zeros((head_count, head_width, head_width), jnp.float32),
        jnp.zeros((head_count,), jnp.float32),
    )
    final, outputs = lax.scan(
        advance, initial, (shaped(queries), shaped(key_rows), shaped(values), decays)
    )
    local_part = outputs[0].reshape(seq_rows, head_count, head_width)
    query_device = outputs[1].reshape(seq_rows, head_count, head_width)
    return (local_part, query_device, final[0], final[1])


def combine_states(before, after):
    return (before[0] * after[0], after[0][:, None, None] * before[1] + after[1])


def body(tokens, w_query, w_key, w_value, w_gate, decay_exponent, forget, norm_gain):
    seq_rows = tokens.shape[0]
    local_width = w_query.shape[1]
    head_count = decay_exponent.shape[0]
    head_width = local_width // head_count
    empty = jnp.zeros((seq_rows, local_width), jnp.float32)
    summed = (empty, empty, empty, empty)
    piece = lax.all_gather(tokens, "mp", axis=1, tiled=True)
    results = []
    for weight, partial_value in zip((w_query, w_key, w_value, w_gate), summed):
        results.append(jnp.dot(piece, weight, preferred_element_type=jnp.float32))
    projected = tuple(results)
    queries = projected[0].astype(jnp.bfloat16)
    key_rows = (projected[1] * DH ** (-0.5)).astype(jnp.bfloat16)
    values = projected[2].astype(jnp.bfloat16)
    gate = projected[3].astype(jnp.bfloat16)
    rate = jnp.log1p(-jnp.exp2(-decay_exponent.astype(jnp.float32)))
    logdecay = rate[None, :] - forget
    local_part, query_device, own_state, own_total = run_blocks(
        queries, key_rows, values, logdecay, head_count, head_width
    )
    prefix = prefix_2(
        (jnp.exp(own_total), own_state),
        "seq",
        combine_states,
        (jnp.ones_like(own_total), jnp.zeros_like(own_state)),
    )
    incoming = prefix[1]
    from_before = jnp.einsum("tha,hab->thb", query_device, incoming)
    output = (local_part + from_before).astype(jnp.bfloat16).reshape(seq_rows, local_width)
    output_float = output.astype(jnp.float32)
    squares = over_copies(jnp.sum(output_float * output_float, axis=1), "mp")
    rstd = lax.rsqrt(squares / (HEADS * DH) + 1e-06)
    gain_here = lax.dynamic_slice_in_dim(
        norm_gain, lax.axis_index("mp") * local_width, local_width, 0
    )
    gated = (
        jax.nn.silu(gate.astype(jnp.float32)) * output_float * rstd[:, None] * gain_here[None, :]
    )
    return lax.all_to_all(gated.astype(jnp.bfloat16), "mp", split_axis=0, concat_axis=1, tiled=True)


def solution(mesh):
    placed = (
        P(("dp", "seq"), "mp"),
        P(None, "mp"),
        P(None, "mp"),
        P(None, "mp"),
        P(None, "mp"),
        P("mp"),
        P(("dp", "seq"), "mp"),
        P(),
    )
    return jax.shard_map(
        body, mesh=mesh, in_specs=placed, out_specs=P(("dp", "seq", "mp"), None), check_vma=False
    )
```

profile of v0, /device:TPU:1, one launch (start us, length us, event | category | flops | bytes accessed | tf_op | source)
XLA Modules:
  0.0 194.3 jit_solution(12837014939397995423)
XLA Ops:
  6.5 0.7 all-gather.2.cloned.1.call-update
  8.0 0.7 broadcast_subtract_fusion
  8.7 76.1 %all-gather.2.cloned.1.call-done = bf16[2048,2048]{1,0:T(8,128)(2,1)} async-done(((bf16[2048,128]{1,0:T(8,128)(2,1)}), bf16[2048,2048]{1,0:T(8,128)(2,1)}) %all-gather.2.cloned.1.call-update) | async-done | bytes 8388624 | tf_op jit(solution)/shard_map/all_gather | solution.py:120
  84.8 5.9 %fusion.52 = bf16[2048,128]{1,0:T(8,128)(2,1)S(1)} fusion(bf16[2048,2048]{1,0:T(8,128)(2,1)} %all-gather.2.cloned.1.call-done, bf16[2048,128]{1,0:T(8,128)(2,1)S(1)} %copy-done), kind=kOutput, calls=%fused_computation.61 | convolution fusion | flops 1074266112 | bytes 9437184 | tf_op jit(solution)/shard_map/dot_general | solution.py:123
  90.7 3.3 %convolution_convert_fusion.1 = bf16[2048,128]{1,0:T(8,128)(2,1)} fusion(bf16[2048,2048]{1,0:T(8,128)(2,1)S(1)} %copy-done.1, bf16[2048,128]{1,0:T(8,128)(2,1)S(1)} %copy-done.2), kind=kOutput, calls=%fused_computation.57 | convolution fusion | flops 1074003968 | bytes 9437184 | tf_op jit(solution)/shard_map/dot_general | solution.py:123
  94.0 2.4 %convolution_convert_fusion = bf16[2048,128]{1,0:T(8,128)(2,1)S(1)} fusion(bf16[2048,2048]{1,0:T(8,128)(2,1)S(1)} %copy-done.1, bf16[2048,128]{1,0:T(8,128)(2,1)S(1)} %copy-done.3), kind=kOutput, calls=%fused_computation.56 | convolution fusion | flops 1074003968 | bytes 9437184 | tf_op jit(solution)/shard_map/dot_general | solution.py:123
  96.4 29.3 %while.18 = (s32[]{:T(128)}, f32[1,128,128]{2,1,0:T(8,128)S(1)}, f32[1]{0:T(128)}, f32[4,512,1,128]{3,1,0,2:T(8,128)S(1)}, bf16[4,512,1,128]{3,1,2,0:T(8,128)(2,...) while((s32[]{:T(128)}, f32[1,128,128]{2,1,0:T(8,128)S(1)}, ...), condition=%wide.region_3.4_spmd.clone.clone, body=%wide.region_0.3_spmd.clone.clone.sunk | while | flops 169935888 | bytes 3247952 | solution.py:101
  96.4 0.3 reduce-window.16
  96.7 0.2 slice_reduce_fusion.2
  96.9 0.2 reduce-window.17
  97.2 0.6 slice.110
  97.8 0.6 slice.109
  99.6 0.3 convolution_bitcast_fusion.4
  99.9 1.5 fusion.91
  101.4 0.1 copy.74
  101.6 1.3 fusion.90
  102.9 0.8 fusion.92
  103.7 0.3 reduce-window.16
  104.0 0.2 slice_reduce_fusion.2
  104.2 0.2 reduce-window.17
  104.5 0.6 slice.110
  105.1 0.6 slice.109
  106.9 0.3 convolution_bitcast_fusion.4
  107.3 1.5 fusion.91
  108.7 0.1 copy.74
  108.9 1.3 fusion.90
  110.2 0.8 fusion.92
  111.0 0.3 reduce-window.16
  111.3 0.2 slice_reduce_fusion.2
  111.5 0.2 reduce-window.17
  111.8 0.6 slice.110
  112.4 0.6 slice.109
  114.3 0.3 convolution_bitcast_fusion.4
  114.6 1.5 fusion.91
  116.0 0.1 copy.74
  116.2 1.3 fusion.90
  117.5 0.8 fusion.92
  118.3 0.3 reduce-window.16
  118.6 0.2 slice_reduce_fusion.2
  118.8 0.2 reduce-window.17
  119.1 0.6 slice.110
  119.7 0.6 slice.109
  121.6 0.3 convolution_bitcast_fusion.4
  121.9 1.5 fusion.91
  123.3 0.1 copy.74
  123.5 1.3 fusion.90
  124.8 0.8 fusion.92
  125.7 0.8 broadcast_in_dim.45
  126.5 4.0 %all-to-all-start = ((bf16[8,129,128]{2,1,0:T(8,128)(2,1)}), bf16[8,129,128]{2,1,0:T(8,128)(2,1)S(1)}, u32[]{:S(2)}, u32[]{:S(2)}) async-start(bf16[8,129,128]{2,1,0:T(8,128)(2,1)} %broadcast_in_dim.45), calls=%async_computation | async-start | bytes 557056 | tf_op jit(solution)/shard_map/all_to_all | solution.py:12
  130.5 12.5 %all-to-all-done = bf16[8,129,128]{2,1,0:T(8,128)(2,1)S(1)} async-done(((bf16[8,129,128]{2,1,0:T(8,128)(2,1)}), bf16[8,129,128]{2,1,0:T(8,128)(2,1)S(1)}, u32[]{:S(2)}, u32[]{:S(2)}) %all-to-all-start) | async-done | bytes 264224 | tf_op jit(solution)/shard_map/all_to_all | solution.py:12
  143.1 0.1 fusion.59
  143.3 0.1 fusion.60
  143.4 0.5 slice.63
  143.9 0.1 select_bitcast_fusion
  144.0 0.1 slice_add_fusion
  144.2 2.1 %multiply_reduce_fusion = (f32[2048]{0:T(1024)S(1)}, f32[2048,128]{1,0:T(8,128)S(1)}) fusion(f32[2048,1,128]{2,0,1:T(8,128)S(1)} %bitcast.167, bf16[2048,128]{1,0:T(8,128)(2,1)} %bitcast.171, f32[2,1,128,128]{3,2,1,0:T(8,128)S(1)} %slice_add_fusion.1, f32[]{:T(128)} %bitcast.12), kind=kOutput, calls=%fused_computation.65 | convolution fusion | flops 68450304 | bytes 2760708 | tf_op jit(solution)/shard_map/tha,hab->thb/dot_general | solution.py:141
  146.3 0.7 broadcast_in_dim.49
  147.0 4.9 %all-to-all-start.1 = ((f32[16,1,2048]{2,1,0:T(1,128)}), f32[16,1,2048]{2,1,0:T(1,128)S(1)}, u32[]{:S(2)}, u32[]{:S(2)}) async-start(f32[16,1,2048]{2,1,0:T(1,128)} %broadcast_in_dim.49), calls=%async_computation.1 | async-start | bytes 262144 | tf_op jit(solution)/shard_map/all_to_all | solution.py:12
  151.9 0.8 dynamic_slice.17
  152.7 8.1 %all-to-all-done.1 = f32[16,1,2048]{2,1,0:T(1,128)S(1)} async-done(((f32[16,1,2048]{2,1,0:T(1,128)}), f32[16,1,2048]{2,1,0:T(1,128)S(1)}, u32[]{:S(2)}, u32[]{:S(2)}) %all-to-all-start.1) | async-done | bytes 131104 | tf_op jit(solution)/shard_map/all_to_all | solution.py:12
  160.8 0.1 reduce_sum.19
  160.9 5.8 %multiply_convert_fusion = bf16[2048,128]{1,0:T(8,128)(2,1)S(1)} fusion(f32[2048,128]{1,0:T(8,128)S(1)} %get-tuple-element.204, bf16[2048,2048]{1,0:T(8,128)(2,1)} %all-gather.2.cloned.1.call-done, bf16[2048,128]{1,0:T(8,128)(2,1)} %param.14, f32[128]{0:T(128)S(1)} %dynamic_slice.17, f32[2048]{0:T(1024)S(1)} %add_rsqrt_fusion), kind=kOutput, calls=%fused_computation.64 | convolution fusion | flops 1076363264 | bytes 10494464 | tf_op jit(solution)/shard_map/dot_general | solution.py:123
  166.7 19.9 %all_to_all.30 = bf16[16,128,128]{2,1,0:T(8,128)(2,1)S(1)} all-to-all(bf16[16,128,128]{2,1,0:T(8,128)(2,1)S(1)} %bitcast.170), channel_id=1, replica_groups=mesh['seq'=8,'mp'=16,'dp'=4] {'mp'}, dimensions={0} | all-to-all | bytes 1048576 | tf_op jit(solution)/shard_map/all_to_all | solution.py:152
  186.6 0.9 copy_bitcast_fusion
  (49 shorter events, 1.0 us)
Async XLA Ops:
  6.5 78.2 %copy-start = (bf16[2048,128]{1,0:T(8,128)(2,1)S(1)}, bf16[2048,128]{1,0:T(8,128)(2,1)}, u32[]{:S(2)}) copy-start(bf16[2048,128]{1,0:T(8,128)(2,1)} %param.12) | copy-start | bytes 1572868
  6.5 84.1 %copy-start.2 = (bf16[2048,128]{1,0:T(8,128)(2,1)S(1)}, bf16[2048,128]{1,0:T(8,128)(2,1)}, u32[]{:S(2)}) copy-start(bf16[2048,128]{1,0:T(8,128)(2,1)} %param.13) | copy-start | bytes 1572868
  6.5 78.2 %all-gather.2.cloned.1.call-start = ((), (), s32[]{:S(2)}) async-start(), calls=%async_computation.3 | async-start | bytes 8912896 | tf_op jit(solution)/shard_map/all_gather | solution.py:120
  84.8 5.9 %copy-start.1 = (bf16[2048,2048]{1,0:T(8,128)(2,1)S(1)}, bf16[2048,2048]{1,0:T(8,128)(2,1)}, u32[]{:S(2)}) copy-start(bf16[2048,2048]{1,0:T(8,128)(2,1)} %all-gather.2.cloned.1.call-done) | copy-start | bytes 25165828
  90.7 3.3 %copy-start.3 = (bf16[2048,128]{1,0:T(8,128)(2,1)S(1)}, bf16[2048,128]{1,0:T(8,128)(2,1)}, u32[]{:S(2)}) copy-start(bf16[2048,128]{1,0:T(8,128)(2,1)} %param.11) | copy-start | bytes 1572868
  126.5 16.6 %all-to-all-start = ((bf16[8,129,128]{2,1,0:T(8,128)(2,1)}), bf16[8,129,128]{2,1,0:T(8,128)(2,1)S(1)}, u32[]{:S(2)}, u32[]{:S(2)}) async-start(bf16[8,129,128]{2,1,0:T(8,128)(2,1)} %broadcast_in_dim.45), calls=%async_computation | async-start | bytes 557056 | tf_op jit(solution)/shard_map/all_to_all | solution.py:12
  147.0 13.8 %all-to-all-start.1 = ((f32[16,1,2048]{2,1,0:T(1,128)}), f32[16,1,2048]{2,1,0:T(1,128)S(1)}, u32[]{:S(2)}, u32[]{:S(2)}) async-start(f32[16,1,2048]{2,1,0:T(1,128)} %broadcast_in_dim.49), calls=%async_computation.1 | async-start | bytes 262144 | tf_op jit(solution)/shard_map/all_to_all | solution.py:12
Sparse Core Ops, SparseCore 0:
  9.4 75.3 all-gather.1
where the time goes:
time: 195 us; the launch traced here: 194 us
  waiting for transfers between devices  97.4 us (50%)
  matrix products  31.5 us (16%)
  blocking collectives  19.9 us (10%)
  between operations  14.3 us (7%)
  local copies, waits for them, and re-layouts  10.2 us (5%)
  starting transfers between devices  8.92 us (5%)
  other arithmetic  6.83 us (4%)
  loops' own time  5.24 us (3%)
    all_gather x1, waiting for transfers between devices, body(): piece = lax.all_gather(tokens, 'mp', axis=1, tiled=True)  76.1 us
    all_to_all x2, waiting for transfers between devices, from_everyone(): return lax.all_to_all(copies, axis, split_axis=0, concat_axis=0, tiled=True)  20.7 us
    all_to_all x1, blocking collectives, body(): lax.all_to_all(gated.astype(jnp.bfloat16), 'mp', split_axis=0, concat_axi...  19.9 us
    dot_general x4, matrix products, body(): results.append(jnp.dot(piece, weight, preferred_element_type=jnp.float32))  17.3 us
    all_to_all x2, starting transfers between devices, from_everyone(): return lax.all_to_all(copies, axis, split_axis=0, concat_axis=0, tiled=True)  8.92 us
    dot_general x4, matrix products, advance(): jnp.einsum('hts,shb->thb', scores, value_blk, preferred_element_type=jnp....  5.87 us
    another operation x1, loops' own time, run_blocks(): lax.scan(advance, initial, (shaped(queries), shaped(key_rows), shaped(val...  5.24 us
    dot_general x4, matrix products, advance(): jnp.einsum('sha,shb->hab', key_scaled, value_blk.astype(jnp.float32))  5.01 us
  transfers between devices with their start and end apart: 3, of which 3 were waited for; matrix products, arithmetic and copies ran while one was open for 1% of the time, Pallas kernels for 0%

commit v1 on v0

v1 whole, which is shorter than its diff:
```python
import jax
import jax.numpy as jnp
from jax import lax
from jax.experimental import pallas as pl
from jax.experimental.pallas import tpu as pltpu
from jax.sharding import PartitionSpec as P

DH = 128
CHIPS = 8
BLOCK = 256
BLOCKS = 8
GROUP = 4
MESH = pl.DeviceIdType.MESH
F32 = jnp.float32
BF16 = jnp.bfloat16
PLACE = {0: 0, 1: 1, 7: 2, 2: 3, 6: 4, 3: 5, 5: 6, 4: 7}
ORDER = [0, 1, 7, 2, 6, 3, 5, 4]


def ring_lists():
    right, left = [], []
    for base in range(0, BLOCKS, GROUP):
        even = [base, base + 2, base + 1, base + 3]
        odd = [base + 1, base + 3, base, base + 2]
        for d in (1, 2, 3):
            right += [(j, d) for j in even]
            left += [(j, d) for j in odd]
        right += [(j, 4) for j in even[:2]]
        left += [(j, 4) for j in odd[:2]]
    return right, left


RIGHT, LEFT = ring_lists()
SENDS = len(RIGHT)


def dot(a, b):
    return jnp.dot(a, b, preferred_element_type=F32)


def dot_t(a, b):
    return lax.dot_general(a, b, (((1,), (1,)), ((), ())), preferred_element_type=F32)


def t_dot(a, b):
    return lax.dot_general(a, b, (((0,), (0,)), ((), ())), preferred_element_type=F32)


def kernel(
    tok_hbm, wq_hbm, wk_hbm, wv_hbm, wg_hbm, logd_ref, gain_ref, out_ref,
    tok, w, decay, kdec, qdec, ends, sg, qd, vb, kb, olocal, states, start, own_state, own_total,
    got_state, got_total, ubuf, ssbuf, obuf, ssgot, carried,
    tok_sem, w_sem, right_sem, left_sem, pair_sem, sent_right, sent_left, sent_pair,
    state_sem, total_sem, state_sent, total_sent, o_sem, ss_sem, o_sent, ss_sent, self_sem,
):
    m = lax.axis_index("mp")
    z = lax.axis_index("seq")
    core = lax.rem(m, 2)
    y = m // 2
    pair = m + 1 - 2 * core
    to_right = lax.rem(m + 2, 16)
    to_left = lax.rem(m + 14, 16)

    barrier = pltpu.get_barrier_semaphore()
    for e in range(1, 16):
        pl.semaphore_signal(barrier, inc=1, device_id={"mp": lax.rem(m + e, 16)}, device_id_type=MESH)
    for e in range(1, 8):
        pl.semaphore_signal(barrier, inc=1, device_id={"seq": lax.rem(z + e, 8)}, device_id_type=MESH)

    def columns(place, of):
        return pl.ds(pl.multiple_of(place * 256 + of * 128, 128), 128)

    own_copy = pltpu.make_async_copy(tok_hbm, tok.at[:, columns(0, core)], tok_sem)
    own_copy.start()
    for r in ORDER:
        source = pl.ds(pl.multiple_of(lax.rem(y + 8 - r, 8) * 256, 256), 256)
        rows = pl.ds(PLACE[r] * 256, 256)
        for n, weight in enumerate((wk_hbm, wv_hbm, wq_hbm, wg_hbm)):
            pltpu.make_async_copy(weight.at[source], w.at[rows, pl.ds(n * 128, 128)], w_sem).start()

    logd = logd_ref[...]
    lane = lax.broadcasted_iota(jnp.int32, (16, 128), 1)
    row = lax.broadcasted_iota(jnp.int32, (16, 128), 0)
    run = logd
    for shift in (1, 2, 4, 8, 16, 32, 64):
        run = run + jnp.where(lane >= shift, pltpu.roll(run, shift, 1), 0.0)
    half_sum = jnp.broadcast_to(run[:, 127:128], (16, 128))
    run = run + jnp.where(row % 2 == 1, pltpu.roll(half_sum, 1, 0), 0.0)
    turned = run.T
    before = jnp.zeros((8, 128), F32)
    for j in range(BLOCKS):
        end = jnp.broadcast_to(run[2 * j + 1 : 2 * j + 2, 127:128], (8, 128))
        ends[0, j] = end
        ends[1, j] = before
        before = before + end
    own_total[...] = before

    pl.semaphore_wait(barrier, 22)
    own_copy.wait()

    def ring_copy(direction, index):
        j, d = (RIGHT if direction > 0 else LEFT)[index]
        source = (d - 1) if direction > 0 else (8 - (d - 1)) % 8
        target = d if direction > 0 else 8 - d
        rows = pl.ds(j * BLOCK, BLOCK)
        return pltpu.make_async_remote_copy(
            src_ref=tok.at[rows, columns(PLACE[source], core)],
            dst_ref=tok.at[rows, columns(PLACE[target], core)],
            send_sem=sent_right if direction > 0 else sent_left,
            recv_sem=(right_sem if direction > 0 else left_sem).at[index],
            device_id={"mp": to_right if direction > 0 else to_left},
            device_id_type=MESH,
        )

    def pair_copy(j, r):
        rows = pl.ds(j * BLOCK, BLOCK)
        spot = tok.at[rows, columns(PLACE[r], core)]
        return pltpu.make_async_remote_copy(
            src_ref=spot, dst_ref=spot, send_sem=sent_pair, recv_sem=pair_sem.at[j],
            device_id={"mp": pair}, device_id_type=MESH,
        )

    for index in range(GROUP):
        ring_copy(1, index).start()
        ring_copy(-1, index).start()
    for j in range(BLOCKS):
        pair_copy(j, 0).start()

    def total_copy(e):
        return pltpu.make_async_remote_copy(
            src_ref=own_total, dst_ref=got_total.at[e - 1], send_sem=total_sent.at[e - 1],
            recv_sem=total_sem.at[e - 1], device_id={"seq": lax.rem(z + e, 8)}, device_id_type=MESH,
        )

    def state_copy(e):
        return pltpu.make_async_remote_copy(
            src_ref=own_state, dst_ref=got_state.at[e - 1], send_sem=state_sent.at[e - 1],
            recv_sem=state_sem.at[e - 1], device_id={"seq": lax.rem(z + e, 8)}, device_id_type=MESH,
        )

    for e in range(1, 8):

        @pl.when(z + e < 8)
        def _():
            total_copy(e).start()

    def make_decay(j):
        rows = pl.ds(j * BLOCK, BLOCK)
        down = jnp.concatenate([turned[:, 2 * j : 2 * j + 1], turned[:, 2 * j + 1 : 2 * j + 2]], axis=0)
        across = jnp.concatenate([run[2 * j : 2 * j + 1], run[2 * j + 1 : 2 * j + 2]], axis=1)
        t = lax.broadcasted_iota(jnp.int32, (BLOCK, BLOCK), 0)
        s = lax.broadcasted_iota(jnp.int32, (BLOCK, BLOCK), 1)
        gap = jnp.where(t >= s, down - across, 0.0)
        decay[j] = jnp.where(t >= s, jnp.exp(gap), 0.0)
        wide = jnp.broadcast_to(down, (BLOCK, DH))
        qdec[rows] = jnp.exp(wide)
        kdec[rows] = jnp.exp(ends[0, j, 0:1] - wide)

    def project_kv(j):
        rows = pl.ds(pl.multiple_of(j * BLOCK, BLOCK), BLOCK)
        both = dot(tok[rows], w[:, 0:256])
        keys = (both[:, :128] * DH**-0.5).astype(BF16)
        values = both[:, 128:].astype(BF16)
        kb[rows] = keys
        vb[rows] = values
        faded = (keys.astype(F32) * kdec[rows]).astype(BF16)
        start[j] = carried[...]
        carried[...] = jnp.exp(ends[0, j, 0:1]) * carried[...] + t_dot(faded, values)

    def project_qg(j):
        rows = pl.ds(pl.multiple_of(j * BLOCK, BLOCK), BLOCK)
        both = dot(tok[rows], w[:, 256:512])
        queries = both[:, :128].astype(BF16)
        gate = both[:, 128:].astype(BF16).astype(F32)
        sg[rows] = gate / (1.0 + jnp.exp(-gate)) * gain_ref[pl.ds(m, 1), :]
        qd[rows] = (queries.astype(F32) * qdec[rows]).astype(BF16)
        scores = (dot_t(queries, kb[rows]) * decay[j]).astype(BF16)
        olocal[rows] = dot(scores, vb[rows])

    def wait_weights():
        pltpu.make_async_copy(w, w, w_sem).wait()

    carried[...] = jnp.zeros_like(carried)
    ready = 14
    for index in range(SENDS):
        for direction in (1, -1):
            ring_copy(direction, index).wait_recv()
            if index + GROUP < SENDS:
                ring_copy(direction, index + GROUP).start()
            j, d = (RIGHT if direction > 0 else LEFT)[index]
            pair_copy(j, d if direction > 0 else 8 - d).start()
        if index < BLOCKS:
            make_decay(index)
        if index == ready:
            wait_weights()
            for j in range(GROUP):
                pltpu.make_async_copy(tok.at[pl.ds(0, BLOCK), pl.ds(0, 1024)], tok.at[pl.ds(0, BLOCK), pl.ds(0, 1024)], pair_sem.at[j]).wait()
        piece = index - ready - 1
        if 0 <= piece < 2 * GROUP:
            (project_qg if piece % 2 else project_kv)(piece // 2)

    for j in range(GROUP, BLOCKS):
        pltpu.make_async_copy(tok.at[pl.ds(0, BLOCK), pl.ds(0, 1024)], tok.at[pl.ds(0, BLOCK), pl.ds(0, 1024)], pair_sem.at[j]).wait()

    def each(lower, upper, run_one):
        def step(j, _):
            run_one(j)
            return 0

        lax.fori_loop(lower, upper, step, 0)

    each(GROUP, BLOCKS, project_kv)
    own_state[...] = carried[...].astype(BF16)
    for e in range(1, 8):

        @pl.when(z + e < 8)
        def _():
            state_copy(e).start()

    each(GROUP, BLOCKS, project_qg)

    carried[...] = jnp.zeros_like(carried)
    states[...] = jnp.zeros_like(states)
    for e in range(1, 8):

        @pl.when(z >= e)
        def _():
            total_copy(e).wait_recv()
            state_copy(e).wait_recv()
            carried[...] += jnp.exp(states[0:1]) * got_state[e - 1].astype(F32)
            states[...] += got_total[e - 1]

    one = jnp.ones((8, 128), BF16)

    def out_copy(j, other, r):
        target = 2 * j + other
        return (
            pltpu.make_async_remote_copy(
                src_ref=ubuf.at[j, pl.ds(pl.multiple_of(other * 128, 128), 128)], dst_ref=obuf.at[m], send_sem=o_sent, recv_sem=o_sem,
                device_id={"mp": target}, device_id_type=MESH,
            ),
            pltpu.make_async_remote_copy(
                src_ref=ssbuf.at[j, other], dst_ref=ssgot.at[m], send_sem=ss_sent, recv_sem=ss_sem,
                device_id={"mp": target}, device_id_type=MESH,
            ),
        )

    for r in (4, 3, 5, 2, 6, 1, 7, 0):
        j = lax.rem(y + r, 8)
        rows = pl.ds(pl.multiple_of(j * BLOCK, BLOCK), BLOCK)
        entering = start[j] + jnp.exp(ends[1, j, 0:1]) * carried[...]
        o = (olocal[rows] + dot(qd[rows], entering.astype(BF16))).astype(BF16).astype(F32)
        ubuf[j] = (sg[rows] * o).astype(BF16)
        square = o * o
        high = square.astype(BF16)
        low = (square - high.astype(F32)).astype(BF16)
        total = dot_t(one, high) + dot_t(one, low)
        ssbuf[j, 0] = total[:, :128]
        ssbuf[j, 1] = total[:, 128:]
        if r:
            for other in (0, 1):
                for copy in out_copy(j, other, r):
                    copy.start()
        else:
            for copy in out_copy(j, 1 - core, r):
                copy.start()
            mine = pl.ds(pl.multiple_of(core * 128, 128), 128)
            keep = (
                pltpu.make_async_copy(ubuf.at[j, mine], obuf.at[m], self_sem.at[0]),
                pltpu.make_async_copy(ssbuf.at[j, core], ssgot.at[m], self_sem.at[1]),
            )
            for copy in keep:
                copy.start()
            for copy in keep:
                copy.wait()

    pltpu.make_async_copy(ssgot.at[pl.ds(0, 15)], ssgot.at[pl.ds(0, 15)], ss_sem).wait()
    pltpu.make_async_copy(obuf.at[pl.ds(0, 15)], obuf.at[pl.ds(0, 15)], o_sem).wait()
    squares = ssgot[0]
    for n in range(1, 16):
        squares = squares + ssgot[n]
    rstd = lax.rsqrt(squares / 2048.0 + 1e-06)
    down = jnp.broadcast_to(rstd[0:1], (128, 128)).T
    for n in range(16):
        out_ref[:, n * 128 : (n + 1) * 128] = (obuf[n].astype(F32) * down).astype(BF16)

    for sem in (sent_right, sent_left):
        spot = tok.at[pl.ds(0, SENDS * 16), :]
        pltpu.make_async_copy(spot, spot, sem).wait()
    spot = tok.at[:, pl.ds(0, 1024)]
    pltpu.make_async_copy(spot, spot, sent_pair).wait()
    pltpu.make_async_copy(obuf.at[pl.ds(0, 15)], obuf.at[pl.ds(0, 15)], o_sent).wait()
    pltpu.make_async_copy(ssgot.at[pl.ds(0, 15)], ssgot.at[pl.ds(0, 15)], ss_sent).wait()
    for e in range(1, 8):

        @pl.when(z + e < 8)
        def _():
            total_copy(e).wait_send()
            state_copy(e).wait_send()


def body(tokens, w_query, w_key, w_value, w_gate, decay_exponent, forget, norm_gain):
    rate = jnp.log1p(-jnp.exp2(-decay_exponent.astype(F32)))
    logd = rate[0] - forget.reshape(16, 128)
    gain = norm_gain.reshape(16, 128)
    vmem = pl.BlockSpec(memory_space=pltpu.VMEM)
    anywhere = pl.BlockSpec(memory_space=pl.ANY)
    dma = pltpu.SemaphoreType.DMA
    return pl.pallas_call(
        kernel,
        out_shape=jax.ShapeDtypeStruct((128, 2048), BF16),
        in_specs=[anywhere] * 5 + [vmem] * 2,
        out_specs=vmem,
        scratch_shapes=[
            pltpu.VMEM((2048, 2048), BF16),
            pltpu.VMEM((2048, 512), BF16),
            pltpu.VMEM((8, BLOCK, BLOCK), F32),
            pltpu.VMEM((2048, 128), F32),
            pltpu.VMEM((2048, 128), F32),
            pltpu.VMEM((2, 8, 8, 128), F32),
            pltpu.VMEM((2048, 128), F32),
            pltpu.VMEM((2048, 128), BF16),
            pltpu.VMEM((2048, 128), BF16),
            pltpu.VMEM((2048, 128), BF16),
            pltpu.VMEM((2048, 128), F32),
            pltpu.VMEM((8, 128), F32),
            pltpu.VMEM((8, 128, 128), F32),
            pltpu.VMEM((128, 128), BF16),
            pltpu.VMEM((8, 128), F32),
            pltpu.VMEM((7, 128, 128), BF16),
            pltpu.VMEM((7, 8, 128), F32),
            pltpu.VMEM((8, BLOCK, 128), BF16),
            pltpu.VMEM((8, 2, 8, 128), F32),
            pltpu.VMEM((16, 128, 128), BF16),
            pltpu.VMEM((16, 8, 128), F32),
            pltpu.VMEM((128, 128), F32),
            dma(()), dma(()), dma((SENDS,)), dma((SENDS,)), dma((8,)), dma(()), dma(()), dma(()),
            dma((7,)), dma((7,)), dma((7,)), dma((7,)), dma(()), dma(()), dma(()), dma(()), dma((2,)),
        ],
        compiler_params=pltpu.CompilerParams(
            collective_id=0, has_side_effects=True, vmem_limit_bytes=66 * 1000 * 1000
        ),
        name="retention_all",
    )(tokens, w_query, w_key, w_value, w_gate, logd, gain)


def solution(mesh):
    placed = (
        P(("dp", "seq"), "mp"),
        P(None, "mp"),
        P(None, "mp"),
        P(None, "mp"),
        P(None, "mp"),
        P("mp"),
        P(("dp", "seq"), "mp"),
        P(),
    )
    return jax.shard_map(
        body, mesh=mesh, in_specs=placed, out_specs=P(("dp", "seq", "mp"), None), check_vma=False
    )
```

time: 195 us -> 82.4 us (0.42)
  waiting for transfers between devices: 97.4 us -> 0 us
  Pallas kernels: 0 us -> 78.3 us
  matrix products: 31.5 us -> 0 us
  blocking collectives: 19.9 us -> 0 us
  between operations: 14.3 us -> 0.75 us
  starting transfers between devices: 8.92 us -> 0 us
  local copies, waits for them, and re-layouts: 10.2 us -> 2.49 us
  other arithmetic: 6.83 us -> 0.6 us
  loops' own time: 5.24 us -> 0 us
    pallas_call x0 -> x1, Pallas kernels: none -> 78.3 us  [body(): pl.pallas_call(kernel, out_shape=jax.ShapeDtypeStruct((128, 2048), BF16),...]
    all_gather x1 -> x0, waiting for transfers between devices: 76.1 us -> none  [body(): piece = lax.all_gather(tokens, 'mp', axis=1, tiled=True)]
    dot_general x17 -> x0, matrix products: 31.5 us -> none  [the longest x4 17.3 us: body(): results.append(jnp.dot(piece, weight, preferred_element_type=jnp.float32))]
    all_to_all x2 -> x0, waiting for transfers between devices: 20.7 us -> none  [from_everyone(): return lax.all_to_all(copies, axis, split_axis=0, concat_axis=0, tiled=True)]
    all_to_all x1 -> x0, blocking collectives: 19.9 us -> none  [body(): lax.all_to_all(gated.astype(jnp.bfloat16), 'mp', split_axis=0, concat_axi...]
    all_to_all x2 -> x0, starting transfers between devices: 8.92 us -> none  [from_everyone(): return lax.all_to_all(copies, axis, split_axis=0, concat_axis=0, tiled=True)]
    slice x18 -> x0, local copies, waits for them, and re-layouts: 6.13 us -> none  [the longest x8 4.8 us: advance(): running[-1]]
    another operation x1 -> x0, loops' own time: 5.24 us -> none  [run_blocks(): lax.scan(advance, initial, (shaped(queries), shaped(key_rows), shaped(val...]
  transfers between devices with their start and end apart: 3 -> 0, of which waited for: 3 -> 0; matrix products, arithmetic and copies ran while one was open for 1% -> 0% of each run, Pallas kernels for 0% -> 0%
where the time goes in v1:
time: 82.4 us; the launch traced here: 82.2 us
  Pallas kernels  78.3 us (95%)
  local copies, waits for them, and re-layouts  2.49 us (3%)
    pallas_call x1, Pallas kernels, body(): pl.pallas_call(kernel, out_shape=jax.ShapeDtypeStruct((128, 2048), BF16),...  78.3 us
    unnamed x3, local copies, waits for them, and re-layouts  2.49 us

profile of v1, /device:TPU:1, one launch (start us, length us, event | category | flops | bytes accessed | tf_op | source)
XLA Modules:
  0.0 82.2 jit_solution(6880893185956552765)
XLA Ops:
  0.7 0.0 copy-start
  0.7 0.6 copy-done
  1.4 0.6 broadcast_subtract_fusion
  2.0 78.3 %retention_all.1 = bf16[128,2048]{1,0:T(8,128)(2,1)} custom-call(bf16[2048,128]{1,0:T(8,128)(2,1)} %tok_hbm.1, bf16[2048,128]{1,0:T(8,128)(2,1)} %wq_hbm.1, bf16[2048,128]{1,0:T(8,128)(2,1)} %wk_hbm.1, bf16[2048,128]{1,0:T(8,128)(2,1)} %wv_hbm.1, bf16[2048,128]{1,0:T(8,128)(2,1)} %wg_hbm.1, f32[16,128]{1,0:T(8,128)} %bitcast.3, f32[16,128]{1,0:T(8,128)} %bitcast.4), custom_call_target="tpu_custom_call" | custom-call | tf_op jit(solution)/shard_map/retention_all/pallas_call | solution.py:309
  80.3 1.9 %copy.11 = bf16[128,2048]{1,0:T(8,128)(2,1)} copy(bf16[128,2048]{1,0:T(8,128)(2,1)} %retention_all.1) | data formatting | bytes 1048576
Async XLA Ops:
  0.7 0.7 copy-start

commit v2 on v1

--- a/solution.py
+++ b/solution.py
@@ -47,11 +47,11 @@
 
 
 def kernel(
-    tok_hbm, wq_hbm, wk_hbm, wv_hbm, wg_hbm, logd_ref, gain_ref, out_ref,
+    tok_hbm, wq_hbm, wk_hbm, wv_hbm, wg_hbm, forget_hbm, exponent_ref, gain_ref, out_ref,
     tok, w, decay, kdec, qdec, ends, sg, qd, vb, kb, olocal, states, start, own_state, own_total,
-    got_state, got_total, ubuf, ssbuf, obuf, ssgot, carried,
+    got_state, got_total, ubuf, ssbuf, obuf, ssgot, carried, forget,
     tok_sem, w_sem, right_sem, left_sem, pair_sem, sent_right, sent_left, sent_pair,
-    state_sem, total_sem, state_sent, total_sent, o_sem, ss_sem, o_sent, ss_sent, self_sem,
+    state_sem, total_sem, state_sent, total_sent, o_sem, ss_sem, o_sent, ss_sent, self_sem, later_in, forget_sem,
 ):
     m = lax.axis_index("mp")
     z = lax.axis_index("seq")
@@ -62,23 +62,33 @@
     to_left = lax.rem(m + 14, 16)
 
     barrier = pltpu.get_barrier_semaphore()
-    for e in range(1, 16):
-        pl.semaphore_signal(barrier, inc=1, device_id={"mp": lax.rem(m + e, 16)}, device_id_type=MESH)
-    for e in range(1, 8):
-        pl.semaphore_signal(barrier, inc=1, device_id={"seq": lax.rem(z + e, 8)}, device_id_type=MESH)
+    for near in (to_left, to_right, pair):
+        pl.semaphore_signal(barrier, inc=1, device_id={"mp": near}, device_id_type=MESH)
+    for e in range(1, 8):
+
+        @pl.when(z + e < 8)
+        def _():
+            pl.semaphore_signal(barrier, inc=1, device_id={"seq": lax.rem(z + e, 8)}, device_id_type=MESH)
 
     def columns(place, of):
         return pl.ds(pl.multiple_of(place * 256 + of * 128, 128), 128)
 
     own_copy = pltpu.make_async_copy(tok_hbm, tok.at[:, columns(0, core)], tok_sem)
     own_copy.start()
+    forget_copy = pltpu.make_async_copy(forget_hbm, forget, forget_sem)
+    forget_copy.start()
     for r in ORDER:
         source = pl.ds(pl.multiple_of(lax.rem(y + 8 - r, 8) * 256, 256), 256)
         rows = pl.ds(PLACE[r] * 256, 256)
         for n, weight in enumerate((wk_hbm, wv_hbm, wq_hbm, wg_hbm)):
             pltpu.make_async_copy(weight.at[source], w.at[rows, pl.ds(n * 128, 128)], w_sem).start()
 
-    logd = logd_ref[...]
+    forget_copy.wait()
+    v = jnp.exp2(jnp.full((16, 128), -exponent_ref[0].astype(F32)))
+    series = jnp.full((16, 128), 1.0 / 8)
+    for n in range(7, 0, -1):
+        series = 1.0 / n + v * series
+    logd = -v * series - forget[...]
     lane = lax.broadcasted_iota(jnp.int32, (16, 128), 1)
     row = lax.broadcasted_iota(jnp.int32, (16, 128), 0)
     run = logd
@@ -95,7 +105,13 @@
         before = before + end
     own_total[...] = before
 
-    pl.semaphore_wait(barrier, 22)
+    pl.semaphore_wait(barrier, 3 + z)
+    for e in range(1, 8):
+
+        @pl.when(z >= e)
+        def _():
+            pl.semaphore_signal(later_in.at[e - 1], inc=1, device_id={"seq": lax.rem(z + 8 - e, 8)}, device_id_type=MESH)
+
     own_copy.wait()
 
     def ring_copy(direction, index):
@@ -138,12 +154,6 @@
             recv_sem=state_sem.at[e - 1], device_id={"seq": lax.rem(z + e, 8)}, device_id_type=MESH,
         )
 
-    for e in range(1, 8):
-
-        @pl.when(z + e < 8)
-        def _():
-            total_copy(e).start()
-
     def make_decay(j):
         rows = pl.ds(j * BLOCK, BLOCK)
         down = jnp.concatenate([turned[:, 2 * j : 2 * j + 1], turned[:, 2 * j + 1 : 2 * j + 2]], axis=0)
@@ -192,6 +202,13 @@
         if index < BLOCKS:
             make_decay(index)
         if index == ready:
+            for e in range(1, 8):
+
+                @pl.when(z + e < 8)
+                def _():
+                    pl.semaphore_wait(later_in.at[e - 1], 1)
+                    total_copy(e).start()
+
             wait_weights()
             for j in range(GROUP):
                 pltpu.make_async_copy(tok.at[pl.ds(0, BLOCK), pl.ds(0, 1024)], tok.at[pl.ds(0, BLOCK), pl.ds(0, 1024)], pair_sem.at[j]).wait()
@@ -300,8 +317,6 @@
 
 
 def body(tokens, w_query, w_key, w_value, w_gate, decay_exponent, forget, norm_gain):
-    rate = jnp.log1p(-jnp.exp2(-decay_exponent.astype(F32)))
-    logd = rate[0] - forget.reshape(16, 128)
     gain = norm_gain.reshape(16, 128)
     vmem = pl.BlockSpec(memory_space=pltpu.VMEM)
     anywhere = pl.BlockSpec(memory_space=pl.ANY)
@@ -309,7 +324,7 @@
     return pl.pallas_call(
         kernel,
         out_shape=jax.ShapeDtypeStruct((128, 2048), BF16),
-        in_specs=[anywhere] * 5 + [vmem] * 2,
+        in_specs=[anywhere] * 6 + [pl.BlockSpec(memory_space=pltpu.SMEM), vmem],
         out_specs=vmem,
         scratch_shapes=[
             pltpu.VMEM((2048, 2048), BF16),
@@ -334,14 +349,16 @@
             pltpu.VMEM((16, 128, 128), BF16),
             pltpu.VMEM((16, 8, 128), F32),
             pltpu.VMEM((128, 128), F32),
+            pltpu.VMEM((16, 128), F32),
             dma(()), dma(()), dma((SENDS,)), dma((SENDS,)), dma((8,)), dma(()), dma(()), dma(()),
             dma((7,)), dma((7,)), dma((7,)), dma((7,)), dma(()), dma(()), dma(()), dma(()), dma((2,)),
+            pltpu.SemaphoreType.REGULAR((7,)), dma(()),
         ],
         compiler_params=pltpu.CompilerParams(
             collective_id=0, has_side_effects=True, vmem_limit_bytes=66 * 1000 * 1000
         ),
         name="retention_all",
-    )(tokens, w_query, w_key, w_value, w_gate, logd, gain)
+    )(tokens, w_query, w_key, w_value, w_gate, forget.reshape(16, 128), decay_exponent, gain)
 
 
 def solution(mesh):

time: 82.4 us -> 77 us (0.934)
  the two profiles are of different devices: /device:TPU:1 before, /device:TPU:455 now
where the time goes in v2:
time: 77 us; the launch traced here: 76.8 us
  Pallas kernels  74.2 us (96%)
  local copies, waits for them, and re-layouts  1.88 us (2%)
    pallas_call x1, Pallas kernels, body(): pl.pallas_call(kernel, out_shape=jax.ShapeDtypeStruct((128, 2048), BF16),...  74.2 us
    unnamed x1, local copies, waits for them, and re-layouts  1.88 us

profile of v2, /device:TPU:455, one launch (start us, length us, event | category | flops | bytes accessed | tf_op | source)
XLA Modules:
  0.0 76.8 jit_solution(7729561087599572871)
XLA Ops:
  0.7 74.2 %retention_all.1 = bf16[128,2048]{1,0:T(8,128)(2,1)} custom-call(bf16[2048,128]{1,0:T(8,128)(2,1)} %tok_hbm.1, bf16[2048,128]{1,0:T(8,128)(2,1)} %wq_hbm.1, bf16[2048,128]{1,0:T(8,128)(2,1)} %wk_hbm.1, bf16[2048,128]{1,0:T(8,128)(2,1)} %wv_hbm.1, bf16[2048,128]{1,0:T(8,128)(2,1)} %wg_hbm.1, f32[16,128]{1,0:T(8,128)} %bitcast.2, s32[1]{0:T(128)S(6)} %copy.10.exponent_ref, ...), custom_call_target="tpu_custom_call" | custom-call | tf_op jit(solution)/shard_map/retention_all/pallas_call | solution.py:324
  74.9 1.9 %copy.11 = bf16[128,2048]{1,0:T(8,128)(2,1)} copy(bf16[128,2048]{1,0:T(8,128)(2,1)} %retention_all.1) | data formatting | bytes 1048576

commit v3 on v2

--- a/solution.py
+++ b/solution.py
@@ -32,6 +32,9 @@
 
 RIGHT, LEFT = ring_lists()
 SENDS = len(RIGHT)
+RIGHT_FIRST = [0, 1, 2, 3, 4, 5, 6, 7]
+PART = {0: 0, 1: 0, 7: 0, 2: 1, 6: 1, 3: 2, 5: 2, 4: 3}
+PLACES = ((0, 3), (3, 5), (5, 7), (7, 8))
 
 
 def dot(a, b):
@@ -49,7 +52,7 @@
 def kernel(
     tok_hbm, wq_hbm, wk_hbm, wv_hbm, wg_hbm, forget_hbm, exponent_ref, gain_ref, out_ref,
     tok, w, decay, kdec, qdec, ends, sg, qd, vb, kb, olocal, states, start, own_state, own_total,
-    got_state, got_total, ubuf, ssbuf, obuf, ssgot, carried, forget,
+    got_state, got_total, ubuf, ssbuf, obuf, ssgot, carried, forget, partial,
     tok_sem, w_sem, right_sem, left_sem, pair_sem, sent_right, sent_left, sent_pair,
     state_sem, total_sem, state_sent, total_sent, o_sem, ss_sem, o_sent, ss_sent, self_sem, later_in, forget_sem,
 ):
@@ -73,8 +76,52 @@
     def columns(place, of):
         return pl.ds(pl.multiple_of(place * 256 + of * 128, 128), 128)
 
-    own_copy = pltpu.make_async_copy(tok_hbm, tok.at[:, columns(0, core)], tok_sem)
-    own_copy.start()
+    def own_copy(j):
+        rows = pl.ds(j * BLOCK, BLOCK)
+        return pltpu.make_async_copy(tok_hbm.at[rows], tok.at[rows, columns(0, core)], tok_sem.at[j])
+
+    for j in RIGHT_FIRST:
+        own_copy(j).start()
+    pl.semaphore_wait(barrier, 3 + z)
+    for e in range(1, 8):
+
+        @pl.when(z >= e)
+        def _():
+            pl.semaphore_signal(later_in.at[e - 1], inc=1, device_id={"seq": lax.rem(z + 8 - e, 8)}, device_id_type=MESH)
+
+
+    def ring_copy(direction, index):
+        j, d = (RIGHT if direction > 0 else LEFT)[index]
+        source = (d - 1) if direction > 0 else (8 - (d - 1)) % 8
+        target = d if direction > 0 else 8 - d
+        rows = pl.ds(j * BLOCK, BLOCK)
+        return pltpu.make_async_remote_copy(
+            src_ref=tok.at[rows, columns(PLACE[source], core)],
+            dst_ref=tok.at[rows, columns(PLACE[target], core)],
+            send_sem=sent_right if direction > 0 else sent_left,
+            recv_sem=(right_sem if direction > 0 else left_sem).at[index],
+            device_id={"mp": to_right if direction > 0 else to_left},
+            device_id_type=MESH,
+        )
+
+    def pair_copy(j, r):
+        rows = pl.ds(j * BLOCK, BLOCK)
+        spot = tok.at[rows, columns(PLACE[r], core)]
+        return pltpu.make_async_remote_copy(
+            src_ref=spot, dst_ref=spot, send_sem=sent_pair, recv_sem=pair_sem.at[j, PART[r]],
+            device_id={"mp": pair}, device_id_type=MESH,
+        )
+
+    for j in range(GROUP):
+        own_copy(j).wait()
+    for index in range(GROUP):
+        ring_copy(1, index).start()
+        ring_copy(-1, index).start()
+    for j in range(GROUP, BLOCKS):
+        own_copy(j).wait()
+    for j in range(BLOCKS):
+        pair_copy(j, 0).start()
+
     forget_copy = pltpu.make_async_copy(forget_hbm, forget, forget_sem)
     forget_copy.start()
     for r in ORDER:
@@ -105,43 +152,6 @@
         before = before + end
     own_total[...] = before
 
-    pl.semaphore_wait(barrier, 3 + z)
-    for e in range(1, 8):
-
-        @pl.when(z >= e)
-        def _():
-            pl.semaphore_signal(later_in.at[e - 1], inc=1, device_id={"seq": lax.rem(z + 8 - e, 8)}, device_id_type=MESH)
-
-    own_copy.wait()
-
-    def ring_copy(direction, index):
-        j, d = (RIGHT if direction > 0 else LEFT)[index]
-        source = (d - 1) if direction > 0 else (8 - (d - 1)) % 8
-        target = d if direction > 0 else 8 - d
-        rows = pl.ds(j * BLOCK, BLOCK)
-        return pltpu.make_async_remote_copy(
-            src_ref=tok.at[rows, columns(PLACE[source], core)],
-            dst_ref=tok.at[rows, columns(PLACE[target], core)],
-            send_sem=sent_right if direction > 0 else sent_left,
-            recv_sem=(right_sem if direction > 0 else left_sem).at[index],
-            device_id={"mp": to_right if direction > 0 else to_left},
-            device_id_type=MESH,
-        )
-
-    def pair_copy(j, r):
-        rows = pl.ds(j * BLOCK, BLOCK)
-        spot = tok.at[rows, columns(PLACE[r], core)]
-        return pltpu.make_async_remote_copy(
-            src_ref=spot, dst_ref=spot, send_sem=sent_pair, recv_sem=pair_sem.at[j],
-            device_id={"mp": pair}, device_id_type=MESH,
-        )
-
-    for index in range(GROUP):
-        ring_copy(1, index).start()
-        ring_copy(-1, index).start()
-    for j in range(BLOCKS):
-        pair_copy(j, 0).start()
-
     def total_copy(e):
         return pltpu.make_async_remote_copy(
             src_ref=own_total, dst_ref=got_total.at[e - 1], send_sem=total_sent.at[e - 1],
@@ -189,6 +199,24 @@
 
     def wait_weights():
         pltpu.make_async_copy(w, w, w_sem).wait()
+
+    def wait_pair(j, part):
+        first, last = PLACES[part]
+        spot = tok.at[pl.ds(j * BLOCK, BLOCK), pl.ds(0, 128 * (last - first))]
+        pltpu.make_async_copy(spot, spot, pair_sem.at[j, part]).wait()
+
+    late = pl.ds(GROUP * BLOCK, GROUP * BLOCK)
+
+    def add_part(j, part):
+        wait_pair(j, part)
+        first, last = PLACES[part]
+        span = pl.ds(first * 256, (last - first) * 256)
+        rows = pl.ds((j - GROUP) * BLOCK, BLOCK)
+        product = dot(tok[pl.ds(j * BLOCK, BLOCK), span], w[span, :])
+        if part:
+            partial[rows] += product
+        else:
+            partial[rows] = product
 
     carried[...] = jnp.zeros_like(carried)
     ready = 14
@@ -211,30 +239,52 @@
 
             wait_weights()
             for j in range(GROUP):
-                pltpu.make_async_copy(tok.at[pl.ds(0, BLOCK), pl.ds(0, 1024)], tok.at[pl.ds(0, BLOCK), pl.ds(0, 1024)], pair_sem.at[j]).wait()
+                for part in range(4):
+                    wait_pair(j, part)
         piece = index - ready - 1
         if 0 <= piece < 2 * GROUP:
             (project_qg if piece % 2 else project_kv)(piece // 2)
+        if 20 <= index < 24:
+            add_part(GROUP + index - 20, 0)
+        if index in (24, 25):
+            add_part(GROUP + 2 * (index - 24), 1)
+            add_part(GROUP + 2 * (index - 24) + 1, 1)
+        if index == 26:
+            for j in range(GROUP, BLOCKS):
+                add_part(j, 2)
 
     for j in range(GROUP, BLOCKS):
-        pltpu.make_async_copy(tok.at[pl.ds(0, BLOCK), pl.ds(0, 1024)], tok.at[pl.ds(0, BLOCK), pl.ds(0, 1024)], pair_sem.at[j]).wait()
-
-    def each(lower, upper, run_one):
-        def step(j, _):
-            run_one(j)
-            return 0
-
-        lax.fori_loop(lower, upper, step, 0)
-
-    each(GROUP, BLOCKS, project_kv)
-    own_state[...] = carried[...].astype(BF16)
+        wait_pair(j, 3)
+    far = tok[late, 1792:2048]
+    both = partial[:, :256] + dot(far, w[1792:2048, :256])
+    keys = (both[:, :128] * DH**-0.5).astype(BF16)
+    values = both[:, 128:].astype(BF16)
+    kb[late] = keys
+    vb[late] = values
+    faded = (keys.astype(F32) * kdec[late]).astype(BF16)
+    added = [
+        t_dot(faded[n * BLOCK : (n + 1) * BLOCK], values[n * BLOCK : (n + 1) * BLOCK]) for n in range(GROUP)
+    ]
+    state = carried[...]
+    for n in range(GROUP):
+        start[GROUP + n] = state
+        state = jnp.exp(ends[0, GROUP + n, 0:1]) * state + added[n]
+    own_state[...] = state.astype(BF16)
     for e in range(1, 8):
 
         @pl.when(z + e < 8)
         def _():
             state_copy(e).start()
 
-    each(GROUP, BLOCKS, project_qg)
+    both = partial[:, 256:] + dot(tok[late, 1792:2048], w[1792:2048, 256:])
+    queries = both[:, :128].astype(BF16)
+    gate = both[:, 128:].astype(BF16).astype(F32)
+    sg[late] = gate / (1.0 + jnp.exp(-gate)) * gain_ref[pl.ds(m, 1), :]
+    qd[late] = (queries.astype(F32) * qdec[late]).astype(BF16)
+    for n in range(GROUP):
+        rows = pl.ds((GROUP + n) * BLOCK, BLOCK)
+        scores = (dot_t(queries[n * BLOCK : (n + 1) * BLOCK], kb[rows]) * decay[GROUP + n]).astype(BF16)
+        olocal[rows] = dot(scores, vb[rows])
 
     carried[...] = jnp.zeros_like(carried)
     states[...] = jnp.zeros_like(states)
@@ -257,7 +307,7 @@
                 device_id={"mp": target}, device_id_type=MESH,
             ),
             pltpu.make_async_remote_copy(
-                src_ref=ssbuf.at[j, other], dst_ref=ssgot.at[m], send_sem=ss_sent, recv_sem=ss_sem,
+                src_ref=ssbuf.at[j, other, pl.ds(0, 1)], dst_ref=ssgot.at[m, pl.ds(0, 1)], send_sem=ss_sent, recv_sem=ss_sem,
                 device_id={"mp": target}, device_id_type=MESH,
             ),
         )
@@ -284,20 +334,20 @@
             mine = pl.ds(pl.multiple_of(core * 128, 128), 128)
             keep = (
                 pltpu.make_async_copy(ubuf.at[j, mine], obuf.at[m], self_sem.at[0]),
-                pltpu.make_async_copy(ssbuf.at[j, core], ssgot.at[m], self_sem.at[1]),
+                pltpu.make_async_copy(ssbuf.at[j, core, pl.ds(0, 1)], ssgot.at[m, pl.ds(0, 1)], self_sem.at[1]),
             )
             for copy in keep:
                 copy.start()
             for copy in keep:
                 copy.wait()
 
-    pltpu.make_async_copy(ssgot.at[pl.ds(0, 15)], ssgot.at[pl.ds(0, 15)], ss_sem).wait()
+    pltpu.make_async_copy(ssgot.at[pl.ds(0, 15), pl.ds(0, 1)], ssgot.at[pl.ds(0, 15), pl.ds(0, 1)], ss_sem).wait()
     pltpu.make_async_copy(obuf.at[pl.ds(0, 15)], obuf.at[pl.ds(0, 15)], o_sem).wait()
-    squares = ssgot[0]
+    squares = ssgot[0, 0:1]
     for n in range(1, 16):
-        squares = squares + ssgot[n]
+        squares = squares + ssgot[n, 0:1]
     rstd = lax.rsqrt(squares / 2048.0 + 1e-06)
-    down = jnp.broadcast_to(rstd[0:1], (128, 128)).T
+    down = jnp.broadcast_to(rstd, (128, 128)).T
     for n in range(16):
         out_ref[:, n * 128 : (n + 1) * 128] = (obuf[n].astype(F32) * down).astype(BF16)
 
@@ -307,7 +357,7 @@
     spot = tok.at[:, pl.ds(0, 1024)]
     pltpu.make_async_copy(spot, spot, sent_pair).wait()
     pltpu.make_async_copy(obuf.at[pl.ds(0, 15)], obuf.at[pl.ds(0, 15)], o_sent).wait()
-    pltpu.make_async_copy(ssgot.at[pl.ds(0, 15)], ssgot.at[pl.ds(0, 15)], ss_sent).wait()
+    pltpu.make_async_copy(ssgot.at[pl.ds(0, 15), pl.ds(0, 1)], ssgot.at[pl.ds(0, 15), pl.ds(0, 1)], ss_sent).wait()
     for e in range(1, 8):
 
         @pl.when(z + e < 8)
@@ -350,7 +400,8 @@
             pltpu.VMEM((16, 8, 128), F32),
             pltpu.VMEM((128, 128), F32),
             pltpu.VMEM((16, 128), F32),
-            dma(()), dma(()), dma((SENDS,)), dma((SENDS,)), dma((8,)), dma(()), dma(()), dma(()),
+            pltpu.VMEM((GROUP * BLOCK, 512), F32),
+            dma((8,)), dma(()), dma((SENDS,)), dma((SENDS,)), dma((8, 4)), dma(()), dma(()), dma(()),
             dma((7,)), dma((7,)), dma((7,)), dma((7,)), dma(()), dma(()), dma(()), dma(()), dma((2,)),
             pltpu.SemaphoreType.REGULAR((7,)), dma(()),
         ],

time: 77 us -> 74.6 us (0.969)
  Pallas kernels: 74.2 us -> 71.7 us
    pallas_call x1, Pallas kernels: 74.2 us -> 71.7 us  [body(): pl.pallas_call(kernel, out_shape=jax.ShapeDtypeStruct((128, 2048), BF16),...]
where the time goes in v3:
time: 74.6 us; the launch traced here: 74.2 us
  Pallas kernels  71.7 us (96%)
  local copies, waits for them, and re-layouts  1.88 us (3%)
    pallas_call x1, Pallas kernels, body(): pl.pallas_call(kernel, out_shape=jax.ShapeDtypeStruct((128, 2048), BF16),...  71.7 us
    unnamed x1, local copies, waits for them, and re-layouts  1.88 us

profile of v3, /device:TPU:455, one launch (start us, length us, event | category | flops | bytes accessed | tf_op | source)
XLA Modules:
  0.0 74.2 jit_solution(15041032528403764532)
XLA Ops:
  0.7 71.7 %retention_all.1 = bf16[128,2048]{1,0:T(8,128)(2,1)} custom-call(bf16[2048,128]{1,0:T(8,128)(2,1)} %tok_hbm.1, bf16[2048,128]{1,0:T(8,128)(2,1)} %wq_hbm.1, bf16[2048,128]{1,0:T(8,128)(2,1)} %wk_hbm.1, bf16[2048,128]{1,0:T(8,128)(2,1)} %wv_hbm.1, bf16[2048,128]{1,0:T(8,128)(2,1)} %wg_hbm.1, f32[16,128]{1,0:T(8,128)} %bitcast.2, s32[1]{0:T(128)S(6)} %copy.10.exponent_ref, ...), custom_call_target="tpu_custom_call" | custom-call | tf_op jit(solution)/shard_map/retention_all/pallas_call | solution.py:374
  72.3 1.9 %copy.11 = bf16[128,2048]{1,0:T(8,128)(2,1)} copy(bf16[128,2048]{1,0:T(8,128)(2,1)} %retention_all.1) | data formatting | bytes 1048576

commit v4 on v3

--- a/solution.py
+++ b/solution.py
@@ -50,11 +50,11 @@
 
 
 def kernel(
-    tok_hbm, wq_hbm, wk_hbm, wv_hbm, wg_hbm, forget_hbm, exponent_ref, gain_ref, out_ref,
+    tok_hbm, wq_hbm, wk_hbm, wv_hbm, wg_hbm, forget_hbm, exponent_ref, gain_hbm, out_ref, down_ref,
     tok, w, decay, kdec, qdec, ends, sg, qd, vb, kb, olocal, states, start, own_state, own_total,
-    got_state, got_total, ubuf, ssbuf, obuf, ssgot, carried, forget, partial,
+    got_state, got_total, ubuf, ssbuf, ssgot, carried, forget, partial, gain_ref,
     tok_sem, w_sem, right_sem, left_sem, pair_sem, sent_right, sent_left, sent_pair,
-    state_sem, total_sem, state_sent, total_sent, o_sem, ss_sem, o_sent, ss_sent, self_sem, later_in, forget_sem,
+    state_sem, total_sem, state_sent, total_sent, o_sem, ss_sem, o_sent, ss_sent, self_sem, later_in, forget_sem, gain_sem,
 ):
     m = lax.axis_index("mp")
     z = lax.axis_index("seq")
@@ -124,6 +124,8 @@
 
     forget_copy = pltpu.make_async_copy(forget_hbm, forget, forget_sem)
     forget_copy.start()
+    gain_copy = pltpu.make_async_copy(gain_hbm, gain_ref, gain_sem)
+    gain_copy.start()
     for r in ORDER:
         source = pl.ds(pl.multiple_of(lax.rem(y + 8 - r, 8) * 256, 256), 256)
         rows = pl.ds(PLACE[r] * 256, 256)
@@ -131,6 +133,7 @@
             pltpu.make_async_copy(weight.at[source], w.at[rows, pl.ds(n * 128, 128)], w_sem).start()
 
     forget_copy.wait()
+    gain_copy.wait()
     v = jnp.exp2(jnp.full((16, 128), -exponent_ref[0].astype(F32)))
     series = jnp.full((16, 128), 1.0 / 8)
     for n in range(7, 0, -1):
@@ -270,7 +273,7 @@
         start[GROUP + n] = state
         state = jnp.exp(ends[0, GROUP + n, 0:1]) * state + added[n]
     own_state[...] = state.astype(BF16)
-    for e in range(1, 8):
+    for e in range(7, 0, -1):
 
         @pl.when(z + e < 8)
         def _():
@@ -303,7 +306,7 @@
         target = 2 * j + other
         return (
             pltpu.make_async_remote_copy(
-                src_ref=ubuf.at[j, pl.ds(pl.multiple_of(other * 128, 128), 128)], dst_ref=obuf.at[m], send_sem=o_sent, recv_sem=o_sem,
+                src_ref=ubuf.at[j, pl.ds(pl.multiple_of(other * 128, 128), 128)], dst_ref=out_ref.at[:, pl.ds(pl.multiple_of(m * 128, 128), 128)], send_sem=o_sent, recv_sem=o_sem,
                 device_id={"mp": target}, device_id_type=MESH,
             ),
             pltpu.make_async_remote_copy(
@@ -333,7 +336,7 @@
                 copy.start()
             mine = pl.ds(pl.multiple_of(core * 128, 128), 128)
             keep = (
-                pltpu.make_async_copy(ubuf.at[j, mine], obuf.at[m], self_sem.at[0]),
+                pltpu.make_async_copy(ubuf.at[j, mine], out_ref.at[:, pl.ds(pl.multiple_of(m * 128, 128), 128)], self_sem.at[0]),
                 pltpu.make_async_copy(ssbuf.at[j, core, pl.ds(0, 1)], ssgot.at[m, pl.ds(0, 1)], self_sem.at[1]),
             )
             for copy in keep:
@@ -342,21 +345,19 @@
                 copy.wait()
 
     pltpu.make_async_copy(ssgot.at[pl.ds(0, 15), pl.ds(0, 1)], ssgot.at[pl.ds(0, 15), pl.ds(0, 1)], ss_sem).wait()
-    pltpu.make_async_copy(obuf.at[pl.ds(0, 15)], obuf.at[pl.ds(0, 15)], o_sem).wait()
+    pltpu.make_async_copy(out_ref.at[:, pl.ds(0, 1920)], out_ref.at[:, pl.ds(0, 1920)], o_sem).wait()
     squares = ssgot[0, 0:1]
     for n in range(1, 16):
         squares = squares + ssgot[n, 0:1]
     rstd = lax.rsqrt(squares / 2048.0 + 1e-06)
-    down = jnp.broadcast_to(rstd, (128, 128)).T
-    for n in range(16):
-        out_ref[:, n * 128 : (n + 1) * 128] = (obuf[n].astype(F32) * down).astype(BF16)
+    down_ref[...] = jnp.broadcast_to(rstd, (128, 128)).T
 
     for sem in (sent_right, sent_left):
         spot = tok.at[pl.ds(0, SENDS * 16), :]
         pltpu.make_async_copy(spot, spot, sem).wait()
     spot = tok.at[:, pl.ds(0, 1024)]
     pltpu.make_async_copy(spot, spot, sent_pair).wait()
-    pltpu.make_async_copy(obuf.at[pl.ds(0, 15)], obuf.at[pl.ds(0, 15)], o_sent).wait()
+    pltpu.make_async_copy(out_ref.at[:, pl.ds(0, 1920)], out_ref.at[:, pl.ds(0, 1920)], o_sent).wait()
     pltpu.make_async_copy(ssgot.at[pl.ds(0, 15), pl.ds(0, 1)], ssgot.at[pl.ds(0, 15), pl.ds(0, 1)], ss_sent).wait()
     for e in range(1, 8):
 
@@ -371,11 +372,11 @@
     vmem = pl.BlockSpec(memory_space=pltpu.VMEM)
     anywhere = pl.BlockSpec(memory_space=pl.ANY)
     dma = pltpu.SemaphoreType.DMA
-    return pl.pallas_call(
+    raw, down = pl.pallas_call(
         kernel,
-        out_shape=jax.ShapeDtypeStruct((128, 2048), BF16),
-        in_specs=[anywhere] * 6 + [pl.BlockSpec(memory_space=pltpu.SMEM), vmem],
-        out_specs=vmem,
+        out_shape=(pltpu.VMEM((128, 2048), BF16), pltpu.VMEM((128, 128), F32)),
+        in_specs=[anywhere] * 6 + [pl.BlockSpec(memory_space=pltpu.SMEM), anywhere],
+        out_specs=(vmem, vmem),
         scratch_shapes=[
             pltpu.VMEM((2048, 2048), BF16),
             pltpu.VMEM((2048, 512), BF16),
@@ -396,20 +397,21 @@
             pltpu.VMEM((7, 8, 128), F32),
             pltpu.VMEM((8, BLOCK, 128), BF16),
             pltpu.VMEM((8, 2, 8, 128), F32),
-            pltpu.VMEM((16, 128, 128), BF16),
             pltpu.VMEM((16, 8, 128), F32),
             pltpu.VMEM((128, 128), F32),
             pltpu.VMEM((16, 128), F32),
             pltpu.VMEM((GROUP * BLOCK, 512), F32),
+            pltpu.VMEM((16, 128), F32),
             dma((8,)), dma(()), dma((SENDS,)), dma((SENDS,)), dma((8, 4)), dma(()), dma(()), dma(()),
             dma((7,)), dma((7,)), dma((7,)), dma((7,)), dma(()), dma(()), dma(()), dma(()), dma((2,)),
-            pltpu.SemaphoreType.REGULAR((7,)), dma(()),
+            pltpu.SemaphoreType.REGULAR((7,)), dma(()), dma(()),
         ],
         compiler_params=pltpu.CompilerParams(
-            collective_id=0, has_side_effects=True, vmem_limit_bytes=66 * 1000 * 1000
+            collective_id=0, has_side_effects=True, vmem_limit_bytes=67043328 - 1100 * 1024
         ),
         name="retention_all",
     )(tokens, w_query, w_key, w_value, w_gate, forget.reshape(16, 128), decay_exponent, gain)
+    return (raw.astype(F32) * down[:, :1]).astype(BF16)
 
 
 def solution(mesh):

time: 74.6 us -> 71.3 us (0.956)
  the two profiles are of different devices: /device:TPU:455 before, /device:TPU:321 now
where the time goes in v4:
time: 71.3 us; the launch traced here: 71.1 us
  Pallas kernels  69.3 us (97%)
  other arithmetic  0.96 us (1%)
    pallas_call x1, Pallas kernels, body(): pl.pallas_call(kernel, out_shape=(pltpu.VMEM((128, 2048), BF16), pltpu.VM...  69.3 us

profile of v4, /device:TPU:321, one launch (start us, length us, event | category | flops | bytes accessed | tf_op | source)
XLA Modules:
  0.0 71.1 jit_solution(2643879458838124831)
XLA Ops:
  0.7 69.3 %retention_all.1 = (bf16[128,2048]{1,0:T(8,128)(2,1)S(1)}, f32[128,128]{1,0:T(8,128)S(1)}) custom-call(bf16[2048,128]{1,0:T(8,128)(2,1)} %tok_hbm.1, bf16[2048,128]{1,0:T(8,128)(2,1)} %wq_hbm.1, bf16[2048,128]{1,0:T(8,128)(2,1)} %wk_hbm.1, bf16[2048,128]{1,0:T(8,128)(2,1)} %wv_hbm.1, bf16[2048,128]{1,0:T(8,128)(2,1)} %wg_hbm.1, f32[16,128]{1,0:T(8,128)} %bitcast.2, ...), custom_call_target="tpu_custom_call" | custom-call | tf_op jit(solution)/shard_map/retention_all/pallas_call | solution.py:375
  70.0 0.1 slice_reduce_fusion
  70.1 1.0 %multiply_convert_fusion = bf16[128,2048]{1,0:T(8,128)(2,1)} fusion(bf16[128,2048]{1,0:T(8,128)(2,1)S(1)} %get-tuple-element.7, f32[128]{0:T(128)S(1)} %slice_reduce_fusion), kind=kLoop, calls=%fused_computation | loop fusion | flops 786432 | bytes 1049088 | tf_op jit(solution)/shard_map/convert_element_type | solution.py:414

commit v5 on v4

--- a/solution.py
+++ b/solution.py
@@ -18,21 +18,19 @@
 
 
 def ring_lists():
-    right, left = [], []
-    for base in range(0, BLOCKS, GROUP):
-        even = [base, base + 2, base + 1, base + 3]
-        odd = [base + 1, base + 3, base, base + 2]
-        for d in (1, 2, 3):
-            right += [(j, d) for j in even]
-            left += [(j, d) for j in odd]
-        right += [(j, 4) for j in even[:2]]
-        left += [(j, 4) for j in odd[:2]]
-    return right, left
+    near, far = [0, 2, 1, 3], [4, 6, 5, 7]
+    order = [(j, 1) for j in near] + [(j, 1) for j in far[:2]]
+    order += [(j, 2) for j in near] + [(j, 1) for j in far[2:]]
+    order += [(j, 3) for j in near] + [(j, 2) for j in far[:2]]
+    order += [(j, 4) for j in near[:2]] + [(j, 2) for j in far[2:]]
+    order += [(j, 3) for j in far] + [(j, 4) for j in far[:2]]
+    return order, [(j + 1 - 2 * (j % 2), d) for j, d in order]
 
 
 RIGHT, LEFT = ring_lists()
+FLIGHT = 6
+START = [max(n - FLIGHT, RIGHT.index((j, d - 1)) if d > 1 else -1) for n, (j, d) in enumerate(RIGHT)]
 SENDS = len(RIGHT)
-RIGHT_FIRST = [0, 1, 2, 3, 4, 5, 6, 7]
 PART = {0: 0, 1: 0, 7: 0, 2: 1, 6: 1, 3: 2, 5: 2, 4: 3}
 PLACES = ((0, 3), (3, 5), (5, 7), (7, 8))
 
@@ -64,6 +62,16 @@
     to_right = lax.rem(m + 2, 16)
     to_left = lax.rem(m + 14, 16)
 
+    def columns(place, of):
+        return pl.ds(pl.multiple_of(place * 256 + of * 128, 128), 128)
+
+    def own_copy(j):
+        rows = pl.ds(j * BLOCK, BLOCK)
+        return pltpu.make_async_copy(tok_hbm.at[rows], tok.at[rows, columns(0, core)], tok_sem.at[j])
+
+    for j in (0, 2, 1, 3, 4, 6, 5, 7):
+        own_copy(j).start()
+
     barrier = pltpu.get_barrier_semaphore()
     for near in (to_left, to_right, pair):
         pl.semaphore_signal(barrier, inc=1, device_id={"mp": near}, device_id_type=MESH)
@@ -72,16 +80,6 @@
         @pl.when(z + e < 8)
         def _():
             pl.semaphore_signal(barrier, inc=1, device_id={"seq": lax.rem(z + e, 8)}, device_id_type=MESH)
-
-    def columns(place, of):
-        return pl.ds(pl.multiple_of(place * 256 + of * 128, 128), 128)
-
-    def own_copy(j):
-        rows = pl.ds(j * BLOCK, BLOCK)
-        return pltpu.make_async_copy(tok_hbm.at[rows], tok.at[rows, columns(0, core)], tok_sem.at[j])
-
-    for j in RIGHT_FIRST:
-        own_copy(j).start()
     pl.semaphore_wait(barrier, 3 + z)
     for e in range(1, 8):
 
@@ -119,6 +117,9 @@
         ring_copy(-1, index).start()
     for j in range(GROUP, BLOCKS):
         own_copy(j).wait()
+    for index in range(GROUP, FLIGHT):
+        ring_copy(1, index).start()
+        ring_copy(-1, index).start()
     for j in range(BLOCKS):
         pair_copy(j, 0).start()
 
@@ -179,60 +180,71 @@
         qdec[rows] = jnp.exp(wide)
         kdec[rows] = jnp.exp(ends[0, j, 0:1] - wide)
 
-    def project_kv(j):
-        rows = pl.ds(pl.multiple_of(j * BLOCK, BLOCK), BLOCK)
-        both = dot(tok[rows], w[:, 0:256])
+    def wait_weights():
+        pltpu.make_async_copy(w, w, w_sem).wait()
+
+    def wait_pair(j, part):
+        first, last = PLACES[part]
+        spot = tok.at[pl.ds(j * BLOCK, BLOCK), pl.ds(0, 128 * (last - first))]
+        pltpu.make_async_copy(spot, spot, pair_sem.at[j, part]).wait()
+
+    def add_part(j, part):
+        wait_pair(j, part)
+        first, last = PLACES[part]
+        span = pl.ds(first * 256, (last - first) * 256)
+        rows = pl.ds(j * BLOCK, BLOCK)
+        product = dot(tok[rows, span], w[span, :])
+        if part:
+            partial[rows] += product
+        else:
+            partial[rows] = product
+
+    def finish_kv(rows, count):
+        both = partial[rows, :256] + dot(tok[rows, 1792:2048], w[1792:2048, :256])
         keys = (both[:, :128] * DH**-0.5).astype(BF16)
         values = both[:, 128:].astype(BF16)
         kb[rows] = keys
         vb[rows] = values
         faded = (keys.astype(F32) * kdec[rows]).astype(BF16)
-        start[j] = carried[...]
-        carried[...] = jnp.exp(ends[0, j, 0:1]) * carried[...] + t_dot(faded, values)
-
-    def project_qg(j):
-        rows = pl.ds(pl.multiple_of(j * BLOCK, BLOCK), BLOCK)
-        both = dot(tok[rows], w[:, 256:512])
+        return [
+            t_dot(faded[n * BLOCK : (n + 1) * BLOCK], values[n * BLOCK : (n + 1) * BLOCK]) for n in range(count)
+        ]
+
+    def finish_qg(rows, block, count):
+        both = partial[rows, 256:] + dot(tok[rows, 1792:2048], w[1792:2048, 256:])
         queries = both[:, :128].astype(BF16)
         gate = both[:, 128:].astype(BF16).astype(F32)
         sg[rows] = gate / (1.0 + jnp.exp(-gate)) * gain_ref[pl.ds(m, 1), :]
         qd[rows] = (queries.astype(F32) * qdec[rows]).astype(BF16)
-        scores = (dot_t(queries, kb[rows]) * decay[j]).astype(BF16)
-        olocal[rows] = dot(scores, vb[rows])
-
-    def wait_weights():
-        pltpu.make_async_copy(w, w, w_sem).wait()
-
-    def wait_pair(j, part):
-        first, last = PLACES[part]
-        spot = tok.at[pl.ds(j * BLOCK, BLOCK), pl.ds(0, 128 * (last - first))]
-        pltpu.make_async_copy(spot, spot, pair_sem.at[j, part]).wait()
-
-    late = pl.ds(GROUP * BLOCK, GROUP * BLOCK)
-
-    def add_part(j, part):
-        wait_pair(j, part)
-        first, last = PLACES[part]
-        span = pl.ds(first * 256, (last - first) * 256)
-        rows = pl.ds((j - GROUP) * BLOCK, BLOCK)
-        product = dot(tok[pl.ds(j * BLOCK, BLOCK), span], w[span, :])
-        if part:
-            partial[rows] += product
-        else:
-            partial[rows] = product
+        for n in range(count):
+            span = pl.ds((block + n) * BLOCK, BLOCK)
+            scores = (dot_t(queries[n * BLOCK : (n + 1) * BLOCK], kb[span]) * decay[block + n]).astype(BF16)
+            olocal[span] = dot(scores, vb[span])
+
+    def two(block):
+        return pl.ds(block * BLOCK, 2 * BLOCK)
+
+    def advance(block, added):
+        state = carried[...]
+        for n, more in enumerate(added):
+            start[block + n] = state
+            state = jnp.exp(ends[0, block + n, 0:1]) * state + more
+        return state
 
     carried[...] = jnp.zeros_like(carried)
-    ready = 14
     for index in range(SENDS):
         for direction in (1, -1):
             ring_copy(direction, index).wait_recv()
-            if index + GROUP < SENDS:
-                ring_copy(direction, index + GROUP).start()
+            for later in range(FLIGHT, SENDS):
+                if START[later] == index:
+                    ring_copy(direction, later).start()
             j, d = (RIGHT if direction > 0 else LEFT)[index]
             pair_copy(j, d if direction > 0 else 8 - d).start()
         if index < BLOCKS:
             make_decay(index)
-        if index == ready:
+        if index == 3:
+            wait_weights()
+        if index == 14:
             for e in range(1, 8):
 
                 @pl.when(z + e < 8)
@@ -240,54 +252,45 @@
                     pl.semaphore_wait(later_in.at[e - 1], 1)
                     total_copy(e).start()
 
-            wait_weights()
-            for j in range(GROUP):
-                for part in range(4):
-                    wait_pair(j, part)
-        piece = index - ready - 1
-        if 0 <= piece < 2 * GROUP:
-            (project_qg if piece % 2 else project_kv)(piece // 2)
-        if 20 <= index < 24:
-            add_part(GROUP + index - 20, 0)
+        if 4 <= index < 8:
+            add_part(index - 4, 0)
+        if index in (10, 11):
+            add_part(2 * index - 20, 1)
+            add_part(2 * index - 19, 1)
+        if 12 <= index < 16:
+            add_part(index - 8, 0)
+        if index in (16, 17):
+            add_part(2 * index - 32, 2)
+            add_part(2 * index - 31, 2)
+        if index in (20, 21):
+            block = 2 * index - 40
+            wait_pair(block, 3)
+            wait_pair(block + 1, 3)
+            carried[...] = advance(block, finish_kv(two(block), 2))
+        if index in (22, 23):
+            add_part(2 * index - 40, 1)
+            add_part(2 * index - 39, 1)
         if index in (24, 25):
-            add_part(GROUP + 2 * (index - 24), 1)
-            add_part(GROUP + 2 * (index - 24) + 1, 1)
+            finish_qg(two(2 * index - 48), 2 * index - 48, 2)
         if index == 26:
             for j in range(GROUP, BLOCKS):
                 add_part(j, 2)
 
-    for j in range(GROUP, BLOCKS):
-        wait_pair(j, 3)
-    far = tok[late, 1792:2048]
-    both = partial[:, :256] + dot(far, w[1792:2048, :256])
-    keys = (both[:, :128] * DH**-0.5).astype(BF16)
-    values = both[:, 128:].astype(BF16)
-    kb[late] = keys
-    vb[late] = values
-    faded = (keys.astype(F32) * kdec[late]).astype(BF16)
-    added = [
-        t_dot(faded[n * BLOCK : (n + 1) * BLOCK], values[n * BLOCK : (n + 1) * BLOCK]) for n in range(GROUP)
-    ]
-    state = carried[...]
-    for n in range(GROUP):
-        start[GROUP + n] = state
-        state = jnp.exp(ends[0, GROUP + n, 0:1]) * state + added[n]
-    own_state[...] = state.astype(BF16)
+    for block in (GROUP, GROUP + 2):
+        wait_pair(block, 3)
+        wait_pair(block + 1, 3)
+        carried[...] = advance(block, finish_kv(two(block), 2))
+    own_state[...] = carried[...].astype(BF16)
     for e in range(7, 0, -1):
 
         @pl.when(z + e < 8)
         def _():
             state_copy(e).start()
 
-    both = partial[:, 256:] + dot(tok[late, 1792:2048], w[1792:2048, 256:])
-    queries = both[:, :128].astype(BF16)
-    gate = both[:, 128:].astype(BF16).astype(F32)
-    sg[late] = gate / (1.0 + jnp.exp(-gate)) * gain_ref[pl.ds(m, 1), :]
-    qd[late] = (queries.astype(F32) * qdec[late]).astype(BF16)
-    for n in range(GROUP):
-        rows = pl.ds((GROUP + n) * BLOCK, BLOCK)
-        scores = (dot_t(queries[n * BLOCK : (n + 1) * BLOCK], kb[rows]) * decay[GROUP + n]).astype(BF16)
-        olocal[rows] = dot(scores, vb[rows])
+    finish_qg(pl.ds(GROUP * BLOCK, GROUP * BLOCK), GROUP, GROUP)
+    for j in range(BLOCKS):
+        rows = pl.ds(j * BLOCK, BLOCK)
+        olocal[rows] += dot(qd[rows], start[j].astype(BF16))
 
     carried[...] = jnp.zeros_like(carried)
     states[...] = jnp.zeros_like(states)
@@ -300,6 +303,7 @@
             carried[...] += jnp.exp(states[0:1]) * got_state[e - 1].astype(F32)
             states[...] += got_total[e - 1]
 
+    entering = carried[...].astype(BF16)
     one = jnp.ones((8, 128), BF16)
 
     def out_copy(j, other, r):
@@ -318,8 +322,7 @@
     for r in (4, 3, 5, 2, 6, 1, 7, 0):
         j = lax.rem(y + r, 8)
         rows = pl.ds(pl.multiple_of(j * BLOCK, BLOCK), BLOCK)
-        entering = start[j] + jnp.exp(ends[1, j, 0:1]) * carried[...]
-        o = (olocal[rows] + dot(qd[rows], entering.astype(BF16))).astype(BF16).astype(F32)
+        o = (olocal[rows] + jnp.exp(ends[1, j, 0:1]) * dot(qd[rows], entering)).astype(BF16).astype(F32)
         ubuf[j] = (sg[rows] * o).astype(BF16)
         square = o * o
         high = square.astype(BF16)
@@ -400,7 +403,7 @@
             pltpu.VMEM((16, 8, 128), F32),
             pltpu.VMEM((128, 128), F32),
             pltpu.VMEM((16, 128), F32),
-            pltpu.VMEM((GROUP * BLOCK, 512), F32),
+            pltpu.VMEM((2048, 512), F32),
             pltpu.VMEM((16, 128), F32),
             dma((8,)), dma(()), dma((SENDS,)), dma((SENDS,)), dma((8, 4)), dma(()), dma(()), dma(()),
             dma((7,)), dma((7,)), dma((7,)), dma((7,)), dma(()), dma(()), dma(()), dma(()), dma((2,)),

time: 71.3 us -> 71.1 us (level)
  no operation moved by 1% of the time
where the time goes in v5:
time: 71.1 us; the launch traced here: 70.8 us
  Pallas kernels  69.1 us (97%)
  other arithmetic  0.96 us (1%)
    pallas_call x1, Pallas kernels, body(): pl.pallas_call(kernel, out_shape=(pltpu.VMEM((128, 2048), BF16), pltpu.VM...  69.1 us

profile of v5, /device:TPU:321, one launch (start us, length us, event | category | flops | bytes accessed | tf_op | source)
XLA Modules:
  0.0 70.8 jit_solution(3077700010862915810)
XLA Ops:
  0.7 69.1 %retention_all.1 = (bf16[128,2048]{1,0:T(8,128)(2,1)S(1)}, f32[128,128]{1,0:T(8,128)S(1)}) custom-call(bf16[2048,128]{1,0:T(8,128)(2,1)} %tok_hbm.1, bf16[2048,128]{1,0:T(8,128)(2,1)} %wq_hbm.1, bf16[2048,128]{1,0:T(8,128)(2,1)} %wk_hbm.1, bf16[2048,128]{1,0:T(8,128)(2,1)} %wv_hbm.1, bf16[2048,128]{1,0:T(8,128)(2,1)} %wg_hbm.1, f32[16,128]{1,0:T(8,128)} %bitcast.2, ...), custom_call_target="tpu_custom_call" | custom-call | tf_op jit(solution)/shard_map/retention_all/pallas_call | solution.py:378
  69.7 0.1 slice_reduce_fusion
  69.8 1.0 %multiply_convert_fusion = bf16[128,2048]{1,0:T(8,128)(2,1)} fusion(bf16[128,2048]{1,0:T(8,128)(2,1)S(1)} %get-tuple-element.7, f32[128]{0:T(128)S(1)} %slice_reduce_fusion), kind=kLoop, calls=%fused_computation | loop fusion | flops 786432 | bytes 1049088 | tf_op jit(solution)/shard_map/convert_element_type | solution.py:417

commit v6 on v5

--- a/solution.py
+++ b/solution.py
@@ -50,7 +50,7 @@
 def kernel(
     tok_hbm, wq_hbm, wk_hbm, wv_hbm, wg_hbm, forget_hbm, exponent_ref, gain_hbm, out_ref, down_ref,
     tok, w, decay, kdec, qdec, ends, sg, qd, vb, kb, olocal, states, start, own_state, own_total,
-    got_state, got_total, ubuf, ssbuf, ssgot, carried, forget, partial, gain_ref,
+    got_state, got_total, ubuf, ssbuf, ssgot, carried, forget, partial, gain_ref, reach,
     tok_sem, w_sem, right_sem, left_sem, pair_sem, sent_right, sent_left, sent_pair,
     state_sem, total_sem, state_sent, total_sent, o_sem, ss_sem, o_sent, ss_sent, self_sem, later_in, forget_sem, gain_sem,
 ):
@@ -69,7 +69,7 @@
         rows = pl.ds(j * BLOCK, BLOCK)
         return pltpu.make_async_copy(tok_hbm.at[rows], tok.at[rows, columns(0, core)], tok_sem.at[j])
 
-    for j in (0, 2, 1, 3, 4, 6, 5, 7):
+    for j in (0, 1, 2, 3, 4, 5, 6, 7):
         own_copy(j).start()
 
     barrier = pltpu.get_barrier_semaphore()
@@ -110,16 +110,16 @@
             device_id={"mp": pair}, device_id_type=MESH,
         )
 
-    for j in range(GROUP):
-        own_copy(j).wait()
-    for index in range(GROUP):
+    unloaded = [0, 1, 2, 3, 4, 5, 6, 7]
+    for index in range(FLIGHT):
+        for j in (RIGHT[index][0], LEFT[index][0]):
+            if j in unloaded:
+                own_copy(j).wait()
+                unloaded.remove(j)
         ring_copy(1, index).start()
         ring_copy(-1, index).start()
-    for j in range(GROUP, BLOCKS):
+    for j in unloaded:
         own_copy(j).wait()
-    for index in range(GROUP, FLIGHT):
-        ring_copy(1, index).start()
-        ring_copy(-1, index).start()
     for j in range(BLOCKS):
         pair_copy(j, 0).start()
 
@@ -221,6 +221,11 @@
             scores = (dot_t(queries[n * BLOCK : (n + 1) * BLOCK], kb[span]) * decay[block + n]).astype(BF16)
             olocal[span] = dot(scores, vb[span])
 
+    def add_local(lower, upper):
+        for j in range(lower, upper):
+            rows = pl.ds(j * BLOCK, BLOCK)
+            olocal[rows] += dot(qd[rows], start[j].astype(BF16))
+
     def two(block):
         return pl.ds(block * BLOCK, 2 * BLOCK)
 
@@ -251,6 +256,16 @@
                 def _():
                     pl.semaphore_wait(later_in.at[e - 1], 1)
                     total_copy(e).start()
+
+        if index == 23:
+            states[...] = jnp.zeros_like(states)
+            for e in range(1, 8):
+
+                @pl.when(z >= e)
+                def _():
+                    total_copy(e).wait_recv()
+                    reach[e - 1] = jnp.exp(states[...])
+                    states[...] += got_total[e - 1]
 
         if 4 <= index < 8:
             add_part(index - 4, 0)
@@ -276,6 +291,8 @@
             for j in range(GROUP, BLOCKS):
                 add_part(j, 2)
 
+    add_local(0, GROUP)
+
     for block in (GROUP, GROUP + 2):
         wait_pair(block, 3)
         wait_pair(block + 1, 3)
@@ -288,20 +305,15 @@
             state_copy(e).start()
 
     finish_qg(pl.ds(GROUP * BLOCK, GROUP * BLOCK), GROUP, GROUP)
-    for j in range(BLOCKS):
-        rows = pl.ds(j * BLOCK, BLOCK)
-        olocal[rows] += dot(qd[rows], start[j].astype(BF16))
+    add_local(GROUP, BLOCKS)
 
     carried[...] = jnp.zeros_like(carried)
-    states[...] = jnp.zeros_like(states)
     for e in range(1, 8):
 
         @pl.when(z >= e)
         def _():
-            total_copy(e).wait_recv()
             state_copy(e).wait_recv()
-            carried[...] += jnp.exp(states[0:1]) * got_state[e - 1].astype(F32)
-            states[...] += got_total[e - 1]
+            carried[...] += reach[e - 1, 0:1] * got_state[e - 1].astype(F32)
 
     entering = carried[...].astype(BF16)
     one = jnp.ones((8, 128), BF16)
@@ -321,16 +333,22 @@
 
     for r in (4, 3, 5, 2, 6, 1, 7, 0):
         j = lax.rem(y + r, 8)
-        rows = pl.ds(pl.multiple_of(j * BLOCK, BLOCK), BLOCK)
-        o = (olocal[rows] + jnp.exp(ends[1, j, 0:1]) * dot(qd[rows], entering)).astype(BF16).astype(F32)
-        ubuf[j] = (sg[rows] * o).astype(BF16)
-        square = o * o
-        high = square.astype(BF16)
-        low = (square - high.astype(F32)).astype(BF16)
-        total = dot_t(one, high) + dot_t(one, low)
-        ssbuf[j, 0] = total[:, :128]
-        ssbuf[j, 1] = total[:, 128:]
-        if r:
+        for part in ((0, 1), (1, 1)) if r == 4 else ((0, 2),):
+            rows = pl.ds(pl.multiple_of(j * BLOCK + part[0] * 128, 128), part[1] * 128)
+            o = (olocal[rows] + jnp.exp(ends[1, j, 0:1]) * dot(qd[rows], entering)).astype(BF16).astype(F32)
+            ubuf[j, pl.ds(part[0] * 128, part[1] * 128)] = (sg[rows] * o).astype(BF16)
+            square = o * o
+            high = square.astype(BF16)
+            low = (square - high.astype(F32)).astype(BF16)
+            total = dot_t(one, high) + dot_t(one, low)
+            for n in range(part[1]):
+                ssbuf[j, part[0] + n] = total[:, n * 128 : (n + 1) * 128]
+            if r == 4:
+                for copy in out_copy(j, part[0], r):
+                    copy.start()
+        if r == 4:
+            pass
+        elif r:
             for other in (0, 1):
                 for copy in out_copy(j, other, r):
                     copy.start()
@@ -405,6 +423,7 @@
             pltpu.VMEM((16, 128), F32),
             pltpu.VMEM((2048, 512), F32),
             pltpu.VMEM((16, 128), F32),
+            pltpu.VMEM((7, 8, 128), F32),
             dma((8,)), dma(()), dma((SENDS,)), dma((SENDS,)), dma((8, 4)), dma(()), dma(()), dma(()),
             dma((7,)), dma((7,)), dma((7,)), dma((7,)), dma(()), dma(()), dma(()), dma(()), dma((2,)),
             pltpu.SemaphoreType.REGULAR((7,)), dma(()), dma(()),

time: 71.1 us -> 71.1 us (level)
  no operation moved by 1% of the time
where the time goes in v6:
time: 71.1 us; the launch traced here: 70.9 us
  Pallas kernels  69.1 us (97%)
  other arithmetic  0.96 us (1%)
    pallas_call x1, Pallas kernels, body(): pl.pallas_call(kernel, out_shape=(pltpu.VMEM((128, 2048), BF16), pltpu.VM...  69.1 us

profile of v6, /device:TPU:321, one launch (start us, length us, event | category | flops | bytes accessed | tf_op | source)
XLA Modules:
  0.0 70.9 jit_solution(3501947181411651404)
XLA Ops:
  0.7 69.1 %retention_all.1 = (bf16[128,2048]{1,0:T(8,128)(2,1)S(1)}, f32[128,128]{1,0:T(8,128)S(1)}) custom-call(bf16[2048,128]{1,0:T(8,128)(2,1)} %tok_hbm.1, bf16[2048,128]{1,0:T(8,128)(2,1)} %wq_hbm.1, bf16[2048,128]{1,0:T(8,128)(2,1)} %wk_hbm.1, bf16[2048,128]{1,0:T(8,128)(2,1)} %wv_hbm.1, bf16[2048,128]{1,0:T(8,128)(2,1)} %wg_hbm.1, f32[16,128]{1,0:T(8,128)} %bitcast.2, ...), custom_call_target="tpu_custom_call" | custom-call | tf_op jit(solution)/shard_map/retention_all/pallas_call | solution.py:396
  69.8 0.1 slice_reduce_fusion
  69.9 1.0 %multiply_convert_fusion = bf16[128,2048]{1,0:T(8,128)(2,1)} fusion(bf16[128,2048]{1,0:T(8,128)(2,1)S(1)} %get-tuple-element.7, f32[128]{0:T(128)S(1)} %slice_reduce_fusion), kind=kLoop, calls=%fused_computation | loop fusion | flops 786432 | bytes 1049088 | tf_op jit(solution)/shard_map/convert_element_type | solution.py:436

commit v7 on v5

--- a/solution.py
+++ b/solution.py
@@ -221,6 +221,11 @@
             scores = (dot_t(queries[n * BLOCK : (n + 1) * BLOCK], kb[span]) * decay[block + n]).astype(BF16)
             olocal[span] = dot(scores, vb[span])
 
+    def add_local(lower, upper):
+        for j in range(lower, upper):
+            rows = pl.ds(j * BLOCK, BLOCK)
+            olocal[rows] += dot(qd[rows], start[j].astype(BF16))
+
     def two(block):
         return pl.ds(block * BLOCK, 2 * BLOCK)
 
@@ -272,6 +277,7 @@
             add_part(2 * index - 39, 1)
         if index in (24, 25):
             finish_qg(two(2 * index - 48), 2 * index - 48, 2)
+            add_local(2 * index - 48, 2 * index - 46)
         if index == 26:
             for j in range(GROUP, BLOCKS):
                 add_part(j, 2)
@@ -288,9 +294,7 @@
             state_copy(e).start()
 
     finish_qg(pl.ds(GROUP * BLOCK, GROUP * BLOCK), GROUP, GROUP)
-    for j in range(BLOCKS):
-        rows = pl.ds(j * BLOCK, BLOCK)
-        olocal[rows] += dot(qd[rows], start[j].astype(BF16))
+    add_local(GROUP, BLOCKS)
 
     carried[...] = jnp.zeros_like(carried)
     states[...] = jnp.zeros_like(states)

time: 71.1 us -> 71.1 us (level)
  no operation moved by 1% of the time
where the time goes in v7:
time: 71.1 us; the launch traced here: 70.8 us
  Pallas kernels  69.1 us (97%)
  other arithmetic  0.96 us (1%)
    pallas_call x1, Pallas kernels, body(): pl.pallas_call(kernel, out_shape=(pltpu.VMEM((128, 2048), BF16), pltpu.VM...  69.1 us

profile of v7, /device:TPU:321, one launch (start us, length us, event | category | flops | bytes accessed | tf_op | source)
XLA Modules:
  0.0 70.8 jit_solution(16793754509383749490)
XLA Ops:
  0.7 69.1 %retention_all.1 = (bf16[128,2048]{1,0:T(8,128)(2,1)S(1)}, f32[128,128]{1,0:T(8,128)S(1)}) custom-call(bf16[2048,128]{1,0:T(8,128)(2,1)} %tok_hbm.1, bf16[2048,128]{1,0:T(8,128)(2,1)} %wq_hbm.1, bf16[2048,128]{1,0:T(8,128)(2,1)} %wk_hbm.1, bf16[2048,128]{1,0:T(8,128)(2,1)} %wv_hbm.1, bf16[2048,128]{1,0:T(8,128)(2,1)} %wg_hbm.1, f32[16,128]{1,0:T(8,128)} %bitcast.2, ...), custom_call_target="tpu_custom_call" | custom-call | tf_op jit(solution)/shard_map/retention_all/pallas_call | solution.py:382
  69.7 0.1 slice_reduce_fusion
  69.8 1.0 %multiply_convert_fusion = bf16[128,2048]{1,0:T(8,128)(2,1)} fusion(bf16[128,2048]{1,0:T(8,128)(2,1)S(1)} %get-tuple-element.7, f32[128]{0:T(128)S(1)} %slice_reduce_fusion), kind=kLoop, calls=%fused_computation | loop fusion | flops 786432 | bytes 1049088 | tf_op jit(solution)/shard_map/convert_element_type | solution.py:421
